TPU v7x, 128 devices: a whole 4x4x4 slice. The times are simulated.
128 devices in a mesh: pair: 32 (over x, y, z_lo), idx: 4 (over z_hi, core).
Axes of the slice: x: 4, y: 4, z: 4 (z_hi: 2, z_lo: 2; z = z_hi * 2 + z_lo), core: 2. Of those that a mesh axis runs over, the one named last changes fastest.
Arguments:
- g2: bfloat16 [512, 512, 2, 1, 512], P('pair', None, None, None, 'idx'), may hold values from -6 to 6
- core_ham: float32 [512, 512], replicated, may hold values from -0.25 to 0.25
- dipole: float32 [512, 512], replicated, may hold values from -0.125 to 0.125
- field: float32 [1], replicated, may hold values from 0.5 to 1.5
- rho: bfloat16 [2, 512, 512], replicated, may hold values from -6 to 6
- factors: bfloat16 [2048, 512, 512], P(None, 'pair', 'idx'), may hold values from -0.046875 to 0.046875
- damping: float32 [512], replicated, may hold values from 0.02 to 0.2
Outputs:
- g2_next: bfloat16 [512, 512, 2, 1, 512], P('pair', None, None, None, 'idx')
All inputs are finite; a program needn't handle non-finite values.
Results may differ from a plain program's by a relative error of at most 0.0056.
Values may be sent and summed in bfloat16 or wider, within the bound.
No kernel may reach another device: no remote copies, remote signals or barrier semaphores. Data moves between devices by JAX's collectives and lax.ppermute only.
A program may use at most 192 MiB of HBM per device.

v0:
```python
import functools

import jax
import jax.numpy as jnp
from jax import lax
from jax.experimental import pallas as pl
from jax.experimental.pallas import tpu as pltpu
from jax.sharding import Mesh, PartitionSpec as P

F32 = jnp.float32
BF16 = jnp.bfloat16


def shape(dims, dtype=BF16):
    return jax.ShapeDtypeStruct(dims, dtype)


def call(body, out, grid, ins, outs, scratch, flops, moved, prefetch=1, **kw):
    return pl.pallas_call(
        body,
        out_shape=out,
        grid_spec=pltpu.PrefetchScalarGridSpec(
            num_scalar_prefetch=prefetch,
            grid=grid,
            in_specs=ins,
            out_specs=outs,
            scratch_shapes=scratch,
        ),
        compiler_params=pltpu.CompilerParams(
            dimension_semantics=("arbitrary",) * len(grid), vmem_limit_bytes=56 << 20
        ),
        cost_estimate=pl.CostEstimate(flops=flops, bytes_accessed=moved, transcendentals=0),
        **kw,
    )


def hold(step, first, count):
    return jnp.clip(step - first, 0, count - 1)


def pick_body(me, g, e0, e1, scr):
    step = pl.program_id(0)
    for sub in range(4):
        for i in range(16):
            scr[pl.ds(i * 40, 32), :] = g[i, sub * 32 : sub * 32 + 32, :].astype(F32)
        for s, e in enumerate((e0, e1)):

            @pl.when(step // 2 == s)
            def _(e=e, sub=sub):
                for c in range(2):
                    for i in range(16):
                        rows = scr[pl.ds(i * 40 + c, 16, stride=2), :]
                        e[c, i, sub * 16 : sub * 16 + 16, :] = rows.astype(BF16)


def pick(me, g, first):
    def where(t, me):
        return jnp.bitwise_xor(me[0], first + t // 2) * 2 + t % 2

    piece = lambda s: pl.BlockSpec((2, 16, 64, 128), lambda t, me: (0, 0, hold(t, 2 * s, 2), 0))
    return call(
        pick_body,
        (shape((2, 16, 128, 128)),) * 2,
        (4,),
        [pl.BlockSpec((16, 128, 128), lambda t, me: (0, where(t, me), 0))],
        (piece(0), piece(1)),
        [pltpu.VMEM((640, 128), F32)],
        1 << 24,
        4 << 20,
    )(me, g)


def deal_body(me, *refs):
    gs, t_out, scr = refs[:4], refs[4], refs[5]
    for sub, g in enumerate(gs):
        for i in range(16):
            scr[pl.ds(i * 40, 32), :] = g[i].astype(F32)
        for kc in range(32):
            t_out[sub, kc] = scr[pl.ds(kc, 16, stride=40), :].astype(BF16)


def side_of(me, other):
    return 1 - me[1] if other else me[1]


def deal(me, g, other):
    def piece(sub):
        at = lambda t, me: (0, (t * 4 + sub) * 2 + side_of(me, other), 0)
        return pl.BlockSpec((16, 32, 128), at)

    return call(
        deal_body,
        shape((16, 32, 16, 128)),
        (4,),
        [piece(sub) for sub in range(4)],
        pl.BlockSpec((4, 32, 16, 128), lambda t, me: (t, 0, 0, 0)),
        [pltpu.VMEM((640, 128), F32)],
        1 << 24,
        4 << 20,
    )(me, g, g, g, g)


def flat_body(me, l, la, scr):
    for q in range(128):
        scr[pl.ds(q * 24, 16), :] = l[q].astype(F32)
    for m in range(16):
        rows = scr[pl.ds(m, 128, stride=24), :]
        la[:, m * 128 : m * 128 + 128] = rows.astype(BF16)


def flat(me, factors):
    return call(
        flat_body,
        shape((2048, 2048)),
        (16,),
        [pl.BlockSpec((128, 16, 128), lambda t, me: (t, 0, 0))],
        pl.BlockSpec((128, 2048), lambda t, me: (t, 0)),
        [pltpu.VMEM((3072, 128), F32)],
        1 << 24,
        16 << 20,
    )(me, factors)


def turn_body(me, la, lt):
    for m in range(8):
        lt[m * 128 : m * 128 + 128, :] = la[:, m * 128 : m * 128 + 128].T


def turn(me, la):
    return call(
        turn_body,
        shape((2048, 2048)),
        (2, 8),
        [pl.BlockSpec((256, 1024), lambda r, t, me: (t, r))],
        pl.BlockSpec((1024, 256), lambda r, t, me: (r, t)),
        [],
        1 << 26,
        16 << 20,
    )(me, la)


def base_body(me, e0, e1, e2, e3, ham, dk, dl, di, out, scr):
    for s, e in enumerate((e0, e1, e2, e3)):
        at = pl.multiple_of(jnp.bitwise_xor(me[0], s) * 128, 128)
        for c in range(2):
            scr[pl.ds(at, 128), c * 128 : c * 128 + 128] = e[c, 0]
    term_k = jnp.dot(ham[...], scr[...], preferred_element_type=F32)
    real = scr[:, :128].astype(F32)
    imag = scr[:, 128:].astype(F32)
    h00 = ham[0:1, 0:1].astype(F32)
    decay = di[0] + dk[...] + dl[...]
    out[0, 0] = real + (h00 * imag - term_k[:, 128:]) - decay * real
    out[1, 0] = imag - (h00 * real - term_k[:, :128]) - decay * imag


def base(me, pieces, ham, dk, dl, di):
    return call(
        base_body,
        shape((2, 16, 512, 128), F32),
        (16,),
        [pl.BlockSpec((2, 1, 128, 128), lambda t, me: (0, t, 0, 0))] * 4
        + [
            pl.BlockSpec((512, 512), lambda t, me: (0, 0)),
            pl.BlockSpec((512, 1), lambda t, me: (0, 0)),
            pl.BlockSpec((1, 128), lambda t, me: (0, 0)),
            pl.BlockSpec((1, 1, 1), lambda t, me: (t, 0, 0)),
        ],
        pl.BlockSpec((2, 1, 512, 128), lambda t, me: (0, t, 0, 0)),
        [pltpu.VMEM((512, 256), BF16)],
        1 << 31,
        12 << 20,
    )(me, *pieces, ham, dk, dl, di)


def project_body(me, la, w0, w1, w2, w3, z, rho, out, scr):
    @pl.when(pl.program_id(0) == 0)
    def _():
        for s, w in enumerate((w0, w1, w2, w3)):
            p = jnp.bitwise_xor(me[0], s)
            at = p // 2 * 512 + p % 2 * 128
            for c in range(2):
                scr[:, pl.ds(pl.multiple_of(at + c * 256, 128), 128)] = w[c]

    zr, zi = z[:, 0:1], z[:, 1:2]
    for n in range(4):
        cols = slice(n // 2 * 256, n // 2 * 256 + 256)
        x = jnp.dot(la[...], scr[:, n * 256 : n * 256 + 256], preferred_element_type=F32)
        rr, ri = rho[0:1, cols], rho[1:2, cols]
        x += zr * ri + zi * rr if n % 2 else zr * rr - zi * ri
        out[:, n * 256 : n * 256 + 256] = x.astype(out.dtype)


def project(me, la, pieces, z, rho, other, dtype):
    def at(t, me):
        half = me[0] % 2
        return ((1 - half if other else half) * 2 + t, 0)

    return call(
        project_body,
        shape((1024, 1024), dtype),
        (2,),
        [pl.BlockSpec((512, 2048), at)]
        + [whole((2, 2048, 128))] * 4
        + [pl.BlockSpec((512, 2), at), whole((2, 512))],
        pl.BlockSpec((512, 1024), lambda t, me: (t, 0)),
        [pltpu.VMEM((2048, 1024), BF16)],
        1 << 32,
        10 << 20,
    )(me, la, *pieces, z, rho)


def whole(dims):
    return pl.BlockSpec(dims, lambda t, me: (0,) * len(dims))


def second_body(far, me, lt, own, oth, w0, w1, w2, w3, ham, o0, o1, wcat, res):
    par = me[0] % 2
    lt_own = lt[:, pl.ds(pl.multiple_of(par * 1024, 128), 1024)]
    lt_oth = lt[:, pl.ds(pl.multiple_of((1 - par) * 1024, 128), 1024)]
    side = me[0] // 2
    side = pl.multiple_of((1 - side if far else side) * 256, 128)
    for c in range(2):
        for s, w in enumerate((w0, w1, w2, w3)):
            at = jnp.bitwise_xor(me[0], s) * 128
            wcat[:, pl.ds(pl.multiple_of(at + c * 512, 128), 128)] = w[c]
        cols = slice(c * 256, c * 256 + 256)
        y = jnp.dot(lt_own, own[:, cols], preferred_element_type=F32)
        y += jnp.dot(lt_oth, oth[:, cols], preferred_element_type=F32)
        y -= jnp.dot(wcat[:, c * 512 : c * 512 + 512], ham[:, pl.ds(side, 256)], preferred_element_type=F32)
        res[:, cols] = y.astype(BF16)
        for s, o in enumerate((o0, o1)):
            at = jnp.bitwise_xor(par, s) * 128 + c * 256
            o[c] = res[:, pl.ds(pl.multiple_of(at, 128), 128)]


def second(me, lt, own, oth, pieces, ham, far, first, steps):
    return call(
        functools.partial(second_body, far),
        (shape((2, steps * 512, 128)),) * 2,
        (steps,),
        [
            pl.BlockSpec((512, 2048), lambda t, me: (t + first, 0)),
            whole((1024, 512)),
            whole((1024, 512)),
        ]
        + [pl.BlockSpec((2, 512, 128), lambda t, me: (0, t + first, 0))] * 4
        + [whole((512, 512))],
        (pl.BlockSpec((2, 512, 128), lambda t, me: (0, t, 0)),) * 2,
        [pltpu.VMEM((512, 1024), BF16), pltpu.VMEM((512, 512), BF16)],
        1 << 31,
        8 << 20,
    )(me, lt, own, oth, *pieces, ham)


def mix_body(me, own, oth, ham, out_own, out_oth):
    low = me[1] == 0
    for j in range(4):
        halves = []
        for kc in (2 * j, 2 * j + 1):
            first = jnp.where(low, own[:, kc], oth[:, kc])
            last = jnp.where(low, oth[:, kc], own[:, kc])
            halves.append(jnp.stack([first, last], axis=1).reshape(512, 128))
        both = jnp.concatenate(halves, axis=1)
        y = jnp.dot(ham[...], both, preferred_element_type=F32).astype(BF16)
        for n, kc in enumerate((2 * j, 2 * j + 1)):
            part = y[:, n * 128 : n * 128 + 128].reshape(16, 2, 16, 128)
            out_own[:, kc] = jnp.where(low, part[:, 0], part[:, 1])
            out_oth[:, kc] = jnp.where(low, part[:, 1], part[:, 0])


def mix(me, own, oth, ham):
    block = pl.BlockSpec((16, 8, 16, 128), lambda t, me: (0, t, 0, 0))
    return call(
        mix_body,
        (shape((16, 32, 16, 128)),) * 2,
        (4,),
        [block, block, whole((512, 512))],
        (block, block),
        [],
        1 << 31,
        8 << 20,
    )(me, own, oth, ham)


def finish_body(me, b, t, v0, v1, v20, v21, v30, v31, *refs):
    out, v, first, scr = refs[-4:]
    for s, pieces in enumerate(((v0,), (v1,), (v20, v21), (v30, v31))):

        @pl.when(pl.program_id(0) == s)
        def _(pieces=pieces):
            first_row = 0
            for piece in pieces:
                v[:, first_row : first_row + piece.shape[1]] = piece[:, :, :, 0]
                first_row += piece.shape[1]

    @pl.loop(0, 4)
    def _(j):
        for c in range(2):
            for k in range(16):
                first[pl.ds((c * 16 + k) * 24, 16), :] = t[j, 2 * k + c].astype(F32)
        for i in range(16):
            real = b[0, i, j, 0] + v[1, i, j].astype(F32)
            imag = b[1, i, j, 0] - v[0, i, j].astype(F32)
            real += first[pl.ds(384 + i, 16, stride=24), :]
            imag -= first[pl.ds(i, 16, stride=24), :]
            scr[pl.ds(i * 40, 16, stride=2), :] = real
            scr[pl.ds(i * 40 + 1, 16, stride=2), :] = imag
        for i in range(16):
            out[i, j, 0] = scr[pl.ds(i * 40, 32), :].astype(BF16)


def finish(me, b, t, pieces, other, so_far):
    def side(s):
        return lambda t, me: (0, 0, jnp.bitwise_xor(me[0], t) if s else 0, side_of(me, other), 0, 0)

    def piece(v):
        return pl.BlockSpec((2, v.shape[1], 4, 1, 16, 128), side(0))

    views = [v.reshape(2, -1, 4, 2, 16, 128) for v in pieces]
    extra = [] if so_far is None else [so_far]
    return call(
        finish_body,
        shape((16, 16, 2, 32, 128)),
        (4,),
        [
            pl.BlockSpec((2, 16, 4, 1, 16, 128), side(1)),
            pl.BlockSpec((4, 32, 16, 128), lambda t, me: (jnp.bitwise_xor(me[0], t), 0, 0, 0)),
        ]
        + [piece(v) for v in views]
        + [pl.BlockSpec(memory_space=pl.ANY)] * len(extra),
        pl.BlockSpec(
            (16, 4, 1, 32, 128),
            lambda t, me: (0, jnp.bitwise_xor(me[0], t), side_of(me, other), 0, 0),
        ),
        [
            pltpu.VMEM((2, 16, 4, 16, 128), BF16),
            pltpu.VMEM((768, 128), F32),
            pltpu.VMEM((640, 128), F32),
        ],
        1 << 24,
        10 << 20,
        input_output_aliases={9: 0} if extra else {},
    )(me, b.reshape(2, 16, 16, 2, 16, 128), t, *views, *extra)


def swap(v, s):
    return lax.ppermute(v, ("zh", "c"), [(d, d ^ s) for d in range(4)])


def across(v, s):
    return lax.ppermute(v, ("zl", "zh"), [(d, d ^ s) for d in range(4)])


def to_owner(v, axes):
    return lax.all_to_all(v, axes, split_axis=0, concat_axis=0, tiled=True)


def per_device(g2, core_ham, dipole, field, rho, factors, damping):
    rows, width, _, _, cols = g2.shape
    plane = ("x", "y")
    pair_at = lax.axis_index(("x", "y", "zl"))
    idx_at = lax.axis_index(("zh", "c"))
    side = lax.axis_index("zl")
    me = jnp.stack([idx_at, side]).astype(jnp.int32)
    g = g2.reshape(rows, width * 2, cols)

    e2, e3 = pick(me, g, 2)
    w2, w3 = swap(e2, 2), swap(e3, 3)
    e0, e1 = pick(me, g, 0)
    w1 = swap(e1, 1)
    e = (e0, e1, e2, e3)
    w = [v.reshape(2, rows * 128, cols) for v in (e0, w1, w2, w3)]
    dealt_oth = deal(me, g, True)
    part_oth = to_owner(dealt_oth, plane)
    part_oth = lax.ppermute(part_oth, "zl", [(0, 1), (1, 0)])
    dealt_own = deal(me, g, False)
    part_own = to_owner(dealt_own, plane)

    hamil = 0.5 * (core_ham + core_ham.T) + field[0] * (0.5 * (dipole + dipole.T))
    ham = hamil.astype(BF16)
    rho_rows = lax.dynamic_slice_in_dim(rho, pair_at * rows, rows, 1)
    rho_local = lax.dynamic_slice_in_dim(rho_rows, idx_at * cols, cols, 2)
    z = lax.dot_general(
        factors, rho_local, (((1, 2), (1, 2)), ((), ())), preferred_element_type=F32
    )
    slab = rho[:, 0, :].astype(F32)
    la = flat(me, factors)
    di = lax.dynamic_slice_in_dim(damping, pair_at * rows, rows, 0) + damping[0]
    dl = lax.dynamic_slice_in_dim(damping, idx_at * cols, cols, 0).reshape(1, cols)
    b = base(me, e, ham, damping.reshape(width, 1), dl, di.reshape(rows, 1, 1))
    lt = turn(me, la)

    theirs = project(me, la, w, z, slab, True, BF16)
    theirs = swap(theirs, 1)
    mine = project(me, la, w, z, slab, False, F32)
    share = (mine + theirs.astype(F32)).astype(BF16).reshape(16, 64, 1024)
    share = to_owner(share, plane)
    share = jnp.sum(share.astype(F32), axis=0).astype(BF16)
    shares = [share] + [across(share, s) for s in (1, 2, 3)]
    aux = sum(v.astype(F32) for v in shares).astype(BF16)

    half = lax.axis_index("zh")
    far = lax.dynamic_slice_in_dim(aux, (1 - half) * 512, 512, 1)
    near = lax.dynamic_slice_in_dim(aux, half * 512, 512, 1)
    far = to_owner(jnp.broadcast_to(far[None], (16, 64, 512)), plane).reshape(1024, 512)
    far_oth = swap(far, 1)
    near = to_owner(jnp.broadcast_to(near[None], (16, 64, 512)), plane).reshape(1024, 512)
    near_oth = swap(near, 1)

    mixed_own, mixed_oth = mix(me, part_own, part_oth, ham)
    mixed_oth = lax.ppermute(mixed_oth, "zl", [(0, 1), (1, 0)])
    term_own = to_owner(mixed_own, plane)
    term_oth = to_owner(mixed_oth, plane)

    out_far = []
    for h in range(2):
        r2, r3 = second(me, lt, far, far_oth, w, ham, True, h, 1 + 2 * h)
        out_far.append((swap(r2, 2), swap(r3, 3)))
    r0, r1 = second(me, lt, near, near_oth, w, ham, False, 0, 4)
    r1 = swap(r1, 1)
    pieces = [r0, r1, *[out_far[h][s] for s in range(2) for h in range(2)]]
    out = finish(me, b, term_own, pieces, False, None)
    out = finish(me, b, term_oth, pieces, True, out)
    return out.reshape(rows, width, 2, 1, cols)


def solution(mesh):
    fine = Mesh(mesh.devices.reshape(4, 4, 2, 2, 2), ("x", "y", "zl", "zh", "c"))
    pair, idx = ("x", "y", "zl"), ("zh", "c")
    placed = (P(pair, None, None, None, idx), P(), P(), P(), P(), P(None, pair, idx), P())
    return jax.shard_map(
        per_device,
        mesh=fine,
        in_specs=placed,
        out_specs=P(pair, None, None, None, idx),
        check_vma=False,
    )
```

profile of v0, /device:TPU:1, one launch (start us, length us, event | category | flops | bytes accessed | tf_op | source)
XLA Modules:
  0.0 371.0 jit_solution(5074748815901812012)
XLA Ops:
  0.6 5.0 %shard_map.73 = (bf16[2,16,128,128]{3,2,1,0:T(8,128)(2,1)}, bf16[2,16,128,128]{3,2,1,0:T(8,128)(2,1)}) custom-call(s32[2]{0:T(128)} %pad_add_fusion.me, bf16[16,1024,128]{2,1,0:T(8,128)(2,1)} %bitcast.50), custom_call_target="tpu_custom_call" | custom-call | flops 16777216 | bytes 4194304 | tf_op jit(solution)/shard_map/pallas_call | solution.py:61
  5.6 1.4 collective-permute-start.2
  7.0 5.0 %shard_map.74 = (bf16[2,16,128,128]{3,2,1,0:T(8,128)(2,1)}, bf16[2,16,128,128]{3,2,1,0:T(8,128)(2,1)}) custom-call(s32[2]{0:T(128)} %pad_add_fusion.me, bf16[16,1024,128]{2,1,0:T(8,128)(2,1)} %bitcast.51), custom_call_target="tpu_custom_call" | custom-call | flops 16777216 | bytes 4194304 | tf_op jit(solution)/shard_map/pallas_call | solution.py:61
  12.0 3.7 collective-permute-start.3
  16.4 14.4 %shard_map.79.la = bf16[2048,2048]{1,0:T(8,128)(2,1)} custom-call(s32[2]{0:T(128)} %pad_add_fusion.me, bf16[2048,16,128]{2,1,0:T(8,128)(2,1)} %l.1), custom_call_target="tpu_custom_call" | custom-call | flops 16777216 | bytes 16777216 | tf_op jit(solution)/shard_map/pallas_call | solution.py:112
  32.2 6.7 %fusion.2.z = f32[2048,2]{1,0:T(8,128)} fusion(bf16[2048,16,128]{2,1,0:T(8,128)(2,1)} %l.1, bf16[2,16,128]{2,1,0:T(8,128)(2,1)S(1)} %constant_dynamic-slice_fusion.2), kind=kOutput, calls=%fused_computation.3 | convolution fusion | flops 16777216 | bytes 8413184 | tf_op jit(solution)/shard_map/dot_general | solution.py:383
  39.5 22.5 %collective-permute-done.4 = bf16[2,16,128,128]{3,2,1,0:T(8,128)(2,1)S(1)} collective-permute-done((bf16[2,16,128,128]{3,2,1,0:T(8,128)(2,1)}, bf16[2,16,128,128]{3,2,1,0:T(8,128)(2,1)S(1)}, u32[]{:S(2)}, u32[]{:S(2)}) %collective-permute-start.4) | collective-permute-done | bytes 1048608 | tf_op jit(solution)/shard_map/ppermute | solution.py:347
  62.9 10.6 %shard_map.82 = bf16[1024,1024]{1,0:T(8,128)(2,1)} custom-call(s32[2]{0:T(128)} %pad_add_fusion.me, bf16[2048,2048]{1,0:T(8,128)(2,1)} %shard_map.79.la, bf16[2,2048,128]{2,1,0:T(8,128)(2,1)} %bitcast.62, bf16[2,2048,128]{2,1,0:T(8,128)(2,1)} %bitcast.67, bf16[2,2048,128]{2,1,0:T(8,128)(2,1)} %bitcast.72, bf16[2,2048,128]{2,1,0:T(8,128)(2,1)} %bitcast.77, ...), custom_call_target="tpu_custom_call" | custom-call | flops 4294967296 | bytes 10485760 | tf_op jit(solution)/shard_map/pallas_call | solution.py:198
  73.9 5.0 %shard_map.77 = bf16[16,32,16,128]{3,2,1,0:T(8,128)(2,1)} custom-call(s32[2]{0:T(128)} %pad_add_fusion.me, bf16[16,1024,128]{2,1,0:T(8,128)(2,1)} %bitcast.52, bf16[16,1024,128]{2,1,0:T(8,128)(2,1)} %bitcast.53, bf16[16,1024,128]{2,1,0:T(8,128)(2,1)} %bitcast.54, bf16[16,1024,128]{2,1,0:T(8,128)(2,1)} %bitcast.55), custom_call_target="tpu_custom_call" | custom-call | flops 16777216 | bytes 4194304 | tf_op jit(solution)/shard_map/pallas_call | solution.py:91
  78.9 6.8 %all-to-all-start.1 = ((bf16[16,32,16,128]{3,2,1,0:T(8,128)(2,1)}), bf16[16,32,16,128]{3,2,1,0:T(8,128)(2,1)S(1)}, u32[]{:S(2)}, u32[]{:S(2)}) async-start(bf16[16,32,16,128]{3,2,1,0:T(8,128)(2,1)} %shard_map.77), calls=%async_computation.1 | async-start | bytes 4194304 | tf_op jit(solution)/shard_map/all_to_all | solution.py:355
  85.6 10.9 %shard_map.81 = f32[1024,1024]{1,0:T(8,128)} custom-call(s32[2]{0:T(128)} %pad_add_fusion.me, bf16[2048,2048]{1,0:T(8,128)(2,1)} %shard_map.79.la, bf16[2,2048,128]{2,1,0:T(8,128)(2,1)} %bitcast.63, bf16[2,2048,128]{2,1,0:T(8,128)(2,1)} %bitcast.68, bf16[2,2048,128]{2,1,0:T(8,128)(2,1)} %bitcast.73, bf16[2,2048,128]{2,1,0:T(8,128)(2,1)} %bitcast.78, ...), custom_call_target="tpu_custom_call" | custom-call | flops 4294967296 | bytes 10485760 | tf_op jit(solution)/shard_map/pallas_call | solution.py:198
  96.6 5.0 %add_convert_fusion = bf16[1024,1024]{1,0:T(8,128)(2,1)} fusion(f32[1024,1024]{1,0:T(8,128)} %shard_map.81, bf16[1024,1024]{1,0:T(8,128)(2,1)} %collective-permute-done.5), kind=kLoop, calls=%fused_computation.2 | loop fusion | flops 3145728 | bytes 8388608 | tf_op jit(solution)/shard_map/convert_element_type | solution.py:396
  101.6 13.2 %all-to-all-done.1 = bf16[16,32,16,128]{3,2,1,0:T(8,128)(2,1)S(1)} async-done(((bf16[16,32,16,128]{3,2,1,0:T(8,128)(2,1)}), bf16[16,32,16,128]{3,2,1,0:T(8,128)(2,1)S(1)}, u32[]{:S(2)}, u32[]{:S(2)}) %all-to-all-start.1) | async-done | bytes 2097184 | tf_op jit(solution)/shard_map/all_to_all | solution.py:355
  114.8 1.3 copy-done.9
  116.1 5.4 %all-to-all-start.3 = ((bf16[16,64,1024]{2,1,0:T(8,128)(2,1)}), bf16[16,64,1024]{2,1,0:T(8,128)(2,1)S(1)}, u32[]{:S(2)}, u32[]{:S(2)}) async-start(bf16[16,64,1024]{2,1,0:T(8,128)(2,1)} %bitcast.85), calls=%async_computation.3 | async-start | bytes 4194304 | tf_op jit(solution)/shard_map/all_to_all | solution.py:355
  121.5 5.0 %shard_map.76 = bf16[16,32,16,128]{3,2,1,0:T(8,128)(2,1)} custom-call(s32[2]{0:T(128)} %pad_add_fusion.me, bf16[16,1024,128]{2,1,0:T(8,128)(2,1)} %bitcast.56, bf16[16,1024,128]{2,1,0:T(8,128)(2,1)} %bitcast.57, bf16[16,1024,128]{2,1,0:T(8,128)(2,1)} %bitcast.58, bf16[16,1024,128]{2,1,0:T(8,128)(2,1)} %bitcast.59), custom_call_target="tpu_custom_call" | custom-call | flops 16777216 | bytes 4194304 | tf_op jit(solution)/shard_map/pallas_call | solution.py:91
  126.5 20.8 %all-to-all-done.3 = bf16[16,64,1024]{2,1,0:T(8,128)(2,1)S(1)} async-done(((bf16[16,64,1024]{2,1,0:T(8,128)(2,1)}), bf16[16,64,1024]{2,1,0:T(8,128)(2,1)S(1)}, u32[]{:S(2)}, u32[]{:S(2)}) %all-to-all-start.3) | async-done | bytes 2097184 | tf_op jit(solution)/shard_map/all_to_all | solution.py:355
  147.2 5.6 %all-to-all-start = ((bf16[16,32,16,128]{3,2,1,0:T(8,128)(2,1)}), bf16[16,32,16,128]{3,2,1,0:T(8,128)(2,1)}, u32[]{:S(2)}, u32[]{:S(2)}) async-start(bf16[16,32,16,128]{3,2,1,0:T(8,128)(2,1)} %shard_map.76), calls=%async_computation | async-start | bytes 4194304 | tf_op jit(solution)/shard_map/all_to_all | solution.py:355
  153.2 2.1 collective-permute-start.6
  156.8 1.8 collective-permute-done.6
  158.6 1.6 collective-permute-done.7
  160.2 1.3 collective-permute-done.8
  161.6 16.3 %all-to-all-done.own = bf16[16,32,16,128]{3,2,1,0:T(8,128)(2,1)} async-done(((bf16[16,32,16,128]{3,2,1,0:T(8,128)(2,1)}), bf16[16,32,16,128]{3,2,1,0:T(8,128)(2,1)}, u32[]{:S(2)}, u32[]{:S(2)}) %all-to-all-start) | async-done | bytes 2097184 | tf_op jit(solution)/shard_map/all_to_all | solution.py:355
  178.0 17.5 %all_to_all.35 = bf16[16,64,512]{2,1,0:T(8,128)(2,1)S(1)} all-to-all(bf16[16,64,512]{2,1,0:T(8,128)(2,1)S(1)} %broadcast_in_dim.5), channel_id=1, replica_groups=mesh['x'=4,'y'=4,'zl'=2,'zh'=2,'c'=2] {'x','y'}, dimensions={0} | all-to-all | bytes 2097152 | tf_op jit(solution)/shard_map/all_to_all | solution.py:355
  196.7 4.5 %all-to-all-start.4 = ((bf16[16,64,512]{2,1,0:T(8,128)(2,1)}), bf16[16,64,512]{2,1,0:T(8,128)(2,1)}, u32[]{:S(2)}, u32[]{:S(2)}) async-start(bf16[16,64,512]{2,1,0:T(8,128)(2,1)} %broadcast_in_dim.4), calls=%async_computation.4 | async-start | bytes 2097152 | tf_op jit(solution)/shard_map/all_to_all | solution.py:355
  201.2 1.4 copy.17
  202.6 1.3 copy.18
  204.5 2.9 fusion.7.ham
  207.4 6.9 %shard_map.78 = (bf16[16,32,16,128]{3,2,1,0:T(8,128)(2,1)}, bf16[16,32,16,128]{3,2,1,0:T(8,128)(2,1)}) custom-call(s32[2]{0:T(128)} %pad_add_fusion.me, bf16[16,32,16,128]{3,2,1,0:T(8,128)(2,1)} %all-to-all-done.own, bf16[16,32,16,128]{3,2,1,0:T(8,128)(2,1)} %collective-permute-done.oth, bf16[512,512]{1,0:T(8,128)(2,1)} %fusion.7.ham), custom_call_target="tpu_custom_call" | custom-call | flops 2147483648 | bytes 8388608 | tf_op jit(solution)/shard_map/pallas_call | solution.py:273
  214.4 6.5 %all-to-all-start.6 = ((bf16[16,32,16,128]{3,2,1,0:T(8,128)(2,1)}), bf16[16,32,16,128]{3,2,1,0:T(8,128)(2,1)S(1)}, u32[]{:S(2)}, u32[]{:S(2)}) async-start(bf16[16,32,16,128]{3,2,1,0:T(8,128)(2,1)} %get-tuple-element.28), calls=%async_computation.6 | async-start | bytes 4194304 | tf_op jit(solution)/shard_map/all_to_all | solution.py:355
  220.9 7.0 %collective-permute-start.9 = (bf16[1024,512]{1,0:T(8,128)(2,1)}, bf16[1024,512]{1,0:T(8,128)(2,1)}, u32[]{:S(2)}, u32[]{:S(2)}) collective-permute-start(bf16[1024,512]{1,0:T(8,128)(2,1)} %bitcast.21.own), channel_id=1, source_target_pairs={{0,1},{1,0},{2,3},{3,2},{4,5},{5,4},{6,7},{7,6},{8,9},{9,8},{10,11... | collective-permute-start | bytes 3145736 | tf_op jit(solution)/shard_map/ppermute | solution.py:347
  228.0 14.0 %all-to-all-done.6.t = bf16[16,32,16,128]{3,2,1,0:T(8,128)(2,1)S(1)} async-done(((bf16[16,32,16,128]{3,2,1,0:T(8,128)(2,1)}), bf16[16,32,16,128]{3,2,1,0:T(8,128)(2,1)S(1)}, u32[]{:S(2)}, u32[]{:S(2)}) %all-to-all-start.6) | async-done | bytes 2097184 | tf_op jit(solution)/shard_map/all_to_all | solution.py:355
  242.0 13.8 %collective-permute-done.1 = bf16[16,32,16,128]{3,2,1,0:T(8,128)(2,1)} collective-permute-done((bf16[16,32,16,128]{3,2,1,0:T(8,128)(2,1)}, bf16[16,32,16,128]{3,2,1,0:T(8,128)(2,1)}, u32[]{:S(2)}, u32[]{:S(2)}) %collective-permute-start.1) | collective-permute-done | bytes 2097184 | tf_op jit(solution)/shard_map/ppermute | solution.py:411
  255.8 6.2 %all-to-all-start.2 = ((bf16[16,32,16,128]{3,2,1,0:T(8,128)(2,1)}), bf16[16,32,16,128]{3,2,1,0:T(8,128)(2,1)S(1)}, u32[]{:S(2)}, u32[]{:S(2)}) async-start(bf16[16,32,16,128]{3,2,1,0:T(8,128)(2,1)} %collective-permute-done.1), calls=%async_computation.2 | async-start | bytes 4194304 | tf_op jit(solution)/shard_map/all_to_all | solution.py:355
  262.0 13.9 %shard_map.80.lt = bf16[2048,2048]{1,0:T(8,128)(2,1)} custom-call(s32[2]{0:T(128)} %pad_add_fusion.me, bf16[2048,2048]{1,0:T(8,128)(2,1)} %shard_map.79.la), custom_call_target="tpu_custom_call" | custom-call | flops 67108864 | bytes 16777216 | tf_op jit(solution)/shard_map/pallas_call | solution.py:130
  275.9 12.2 %shard_map.83 = (bf16[2,2048,128]{2,1,0:T(8,128)(2,1)}, bf16[2,2048,128]{2,1,0:T(8,128)(2,1)}) custom-call(s32[2]{0:T(128)} %pad_add_fusion.me, bf16[2048,2048]{1,0:T(8,128)(2,1)} %shard_map.80.lt, bf16[1024,512]{1,0:T(8,128)(2,1)} %bitcast.21.own, bf16[1024,512]{1,0:T(8,128)(2,1)} %collective-permute-done.9.oth, bf16[2,2048,128]{2,1,0:T(8,128)(2,1)} %bitcast.64, ...), custom_call_target="tpu_custom_call" | custom-call | flops 2147483648 | bytes 8388608 | tf_op jit(solution)/shard_map/pallas_call | solution.py:237
  288.1 7.5 %collective-permute-start.10 = (bf16[2,2048,128]{2,1,0:T(8,128)(2,1)}, bf16[2,2048,128]{2,1,0:T(8,128)(2,1)}, u32[]{:S(2)}, u32[]{:S(2)}) collective-permute-start(bf16[2,2048,128]{2,1,0:T(8,128)(2,1)} %get-tuple-element.23), channel_id=1, source_target_pairs={{0,1},{1,0},{2,3},{3,2},{4,5},{5,4},{6,7},{7,6},{8,9},{9,8},{10,11... | collective-permute-start | bytes 3145736 | tf_op jit(solution)/shard_map/ppermute | solution.py:347
  295.7 10.4 %shard_map.85 = (bf16[2,1536,128]{2,1,0:T(8,128)(2,1)}, bf16[2,1536,128]{2,1,0:T(8,128)(2,1)}) custom-call(s32[2]{0:T(128)} %pad_add_fusion.me, bf16[2048,2048]{1,0:T(8,128)(2,1)} %shard_map.80.lt, bf16[1024,512]{1,0:T(8,128)(2,1)} %bitcast.83, bf16[1024,512]{1,0:T(8,128)(2,1)} %collective-permute-done.11.oth, bf16[2,2048,128]{2,1,0:T(8,128)(2,1)} %bitcast.65, ...), custom_call_target="tpu_custom_call" | custom-call | flops 2147483648 | bytes 8388608 | tf_op jit(solution)/shard_map/pallas_call | solution.py:237
  306.0 2.0 collective-permute-start.13
  311.9 6.1 %shard_map.84 = (bf16[2,512,128]{2,1,0:T(8,128)(2,1)}, bf16[2,512,128]{2,1,0:T(8,128)(2,1)}) custom-call(s32[2]{0:T(128)} %pad_add_fusion.me, bf16[2048,2048]{1,0:T(8,128)(2,1)} %shard_map.80.lt, bf16[1024,512]{1,0:T(8,128)(2,1)} %bitcast.84, bf16[1024,512]{1,0:T(8,128)(2,1)} %collective-permute-done.11.oth, bf16[2,2048,128]{2,1,0:T(8,128)(2,1)} %bitcast.66, ...), custom_call_target="tpu_custom_call" | custom-call | flops 2147483648 | bytes 8388608 | tf_op jit(solution)/shard_map/pallas_call | solution.py:237
  318.0 2.0 collective-permute-start.12
  320.0 1.4 collective-permute-start.14
  322.0 14.5 %shard_map.75 = f32[2,16,512,128]{3,2,1,0:T(8,128)} custom-call(s32[2]{0:T(128)} %pad_add_fusion.me, bf16[2,16,128,128]{3,2,1,0:T(8,128)(2,1)} %get-tuple-element.17.e0, bf16[2,16,128,128]{3,2,1,0:T(8,128)(2,1)} %get-tuple-element.18.e1, bf16[2,16,128,128]{3,2,1,0:T(8,128)(2,1)} %get-tuple-element.19.e2, bf16[2,16,128,128]{3,2,1,0:T(8,128)(2,1)} %get-tuple-element.20.e3, ...), custom_call_target="tpu_custom_call" | custom-call | flops 2147483648 | bytes 12582912 | tf_op jit(solution)/shard_map/pallas_call | solution.py:157
  336.5 12.8 %collective-permute-done.12 = bf16[2,512,128]{2,1,0:T(8,128)(2,1)S(1)} collective-permute-done((bf16[2,512,128]{2,1,0:T(8,128)(2,1)}, bf16[2,512,128]{2,1,0:T(8,128)(2,1)S(1)}, u32[]{:S(2)}, u32[]{:S(2)}) %collective-permute-start.12) | collective-permute-done | bytes 262176 | tf_op jit(solution)/shard_map/ppermute | solution.py:347
  349.3 5.8 %collective-permute-done.14 = bf16[2,512,128]{2,1,0:T(8,128)(2,1)S(1)} collective-permute-done((bf16[2,512,128]{2,1,0:T(8,128)(2,1)}, bf16[2,512,128]{2,1,0:T(8,128)(2,1)S(1)}, u32[]{:S(2)}, u32[]{:S(2)}) %collective-permute-start.14) | collective-permute-done | bytes 262176 | tf_op jit(solution)/shard_map/ppermute | solution.py:347
  356.1 6.8 %shard_map.86.refs_0_ = bf16[16,16,2,32,128]{4,3,2,1,0:T(8,128)(2,1)} custom-call(s32[2]{0:T(128)} %pad_add_fusion.me, f32[2,16,16,2,16,128]{5,4,3,2,1,0:T(8,128)} %bitcast.60, bf16[16,32,16,128]{3,2,1,0:T(8,128)(2,1)} %copy-done.5, bf16[2,16,4,2,16,128]{5,4,3,2,1,0:T(8,128)(2,1)} %bitcast.86, bf16[2,16,4,2,16,128]{5,4,3,2,1,0:T(8,128)(2,1)} %bitcast.23.v1, ...), custom_call_target="tpu_custom_call" | custom-call | flops 16777216 | bytes 10485760 | tf_op jit(solution)/shard_map/pallas_call | solution.py:321
  362.9 1.3 copy-done.4
  364.2 6.8 %shard_map.87 = bf16[16,16,2,32,128]{4,3,2,1,0:T(8,128)(2,1)} custom-call(s32[2]{0:T(128)} %pad_add_fusion.me, f32[2,16,16,2,16,128]{5,4,3,2,1,0:T(8,128)} %bitcast.61, bf16[16,32,16,128]{3,2,1,0:T(8,128)(2,1)} %copy-done.4, bf16[2,16,4,2,16,128]{5,4,3,2,1,0:T(8,128)(2,1)} %bitcast.87, ...), custom_call_target="tpu_custom_call", output_to_operand_aliasing={{}: (9, {})} | custom-call | flops 16777216 | bytes 10485760 | tf_op jit(solution)/shard_map/pallas_call | solution.py:321
  (57 shorter events, 13.6 us)
Async XLA Ops:
  5.6 33.3 %collective-permute-start.2 = (bf16[2,16,128,128]{3,2,1,0:T(8,128)(2,1)}, bf16[2,16,128,128]{3,2,1,0:T(8,128)(2,1)S(1)}, u32[]{:S(2)}, u32[]{:S(2)}) collective-permute-start(bf16[2,16,128,128]{3,2,1,0:T(8,128)(2,1)} %get-tuple-element.18.e1), channel_id=1, source_target_pairs={{0,1},{1,0},{2,3},{3,2},{4,5},{5,4},{6,7},{7,6},{8,9},{9,8},{10,11... | collective-permute-start | bytes 3145736 | tf_op jit(solution)/shard_map/ppermute | solution.py:347
  12.0 27.4 %collective-permute-start.3 = (bf16[2,16,128,128]{3,2,1,0:T(8,128)(2,1)}, bf16[2,16,128,128]{3,2,1,0:T(8,128)(2,1)S(1)}, u32[]{:S(2)}, u32[]{:S(2)}) collective-permute-start(bf16[2,16,128,128]{3,2,1,0:T(8,128)(2,1)} %get-tuple-element.19.e2), channel_id=1, source_target_pairs={{0,2},{1,3},{2,0},{3,1},{4,6},{5,7},{6,4},{7,5},{8,10},{9,11},{10,... | collective-permute-start | bytes 3145736 | tf_op jit(solution)/shard_map/ppermute | solution.py:347
  15.7 46.2 %collective-permute-start.4 = (bf16[2,16,128,128]{3,2,1,0:T(8,128)(2,1)}, bf16[2,16,128,128]{3,2,1,0:T(8,128)(2,1)S(1)}, u32[]{:S(2)}, u32[]{:S(2)}) collective-permute-start(bf16[2,16,128,128]{3,2,1,0:T(8,128)(2,1)} %get-tuple-element.20.e3), channel_id=1, source_target_pairs={{0,3},{1,2},{2,1},{3,0},{4,7},{5,6},{6,5},{7,4},{8,11},{9,10},{10,... | collective-permute-start | bytes 3145736 | tf_op jit(solution)/shard_map/ppermute | solution.py:347
  39.0 23.0 %copy-start = (bf16[2,16,128,128]{3,2,1,0:T(8,128)(2,1)}, bf16[2,16,128,128]{3,2,1,0:T(8,128)(2,1)S(1)}, u32[]{:S(2)}) copy-start(bf16[2,16,128,128]{3,2,1,0:T(8,128)(2,1)S(1)} %collective-permute-done.2) | copy-start | bytes 3145732
  39.5 22.5 %copy-start.1 = (bf16[2,16,128,128]{3,2,1,0:T(8,128)(2,1)}, bf16[2,16,128,128]{3,2,1,0:T(8,128)(2,1)S(1)}, u32[]{:S(2)}) copy-start(bf16[2,16,128,128]{3,2,1,0:T(8,128)(2,1)S(1)} %collective-permute-done.3) | copy-start | bytes 3145732
  61.9 1.0 copy-start.2
  73.5 23.1 %collective-permute-start.5 = (bf16[1024,1024]{1,0:T(8,128)(2,1)}, bf16[1024,1024]{1,0:T(8,128)(2,1)}, u32[]{:S(2)}, u32[]{:S(2)}) collective-permute-start(bf16[1024,1024]{1,0:T(8,128)(2,1)} %shard_map.82), channel_id=1, source_target_pairs={{0,1},{1,0},{2,3},{3,2},{4,5},{5,4},{6,7},{7,6},{8,9},{9,8},{10,11... | collective-permute-start | bytes 6291464 | tf_op jit(solution)/shard_map/ppermute | solution.py:347
  78.9 35.9 %all-to-all-start.1 = ((bf16[16,32,16,128]{3,2,1,0:T(8,128)(2,1)}), bf16[16,32,16,128]{3,2,1,0:T(8,128)(2,1)S(1)}, u32[]{:S(2)}, u32[]{:S(2)}) async-start(bf16[16,32,16,128]{3,2,1,0:T(8,128)(2,1)} %shard_map.77), calls=%async_computation.1 | async-start | bytes 4194304 | tf_op jit(solution)/shard_map/all_to_all | solution.py:355
  114.8 1.3 copy-start.9
  116.1 31.2 %all-to-all-start.3 = ((bf16[16,64,1024]{2,1,0:T(8,128)(2,1)}), bf16[16,64,1024]{2,1,0:T(8,128)(2,1)S(1)}, u32[]{:S(2)}, u32[]{:S(2)}) async-start(bf16[16,64,1024]{2,1,0:T(8,128)(2,1)} %bitcast.85), calls=%async_computation.3 | async-start | bytes 4194304 | tf_op jit(solution)/shard_map/all_to_all | solution.py:355
  147.2 30.7 %all-to-all-start = ((bf16[16,32,16,128]{3,2,1,0:T(8,128)(2,1)}), bf16[16,32,16,128]{3,2,1,0:T(8,128)(2,1)}, u32[]{:S(2)}, u32[]{:S(2)}) async-start(bf16[16,32,16,128]{3,2,1,0:T(8,128)(2,1)} %shard_map.76), calls=%async_computation | async-start | bytes 4194304 | tf_op jit(solution)/shard_map/all_to_all | solution.py:355
  153.2 5.4 %collective-permute-start.6 = (bf16[64,1024]{1,0:T(8,128)(2,1)S(1)}, bf16[64,1024]{1,0:T(8,128)(2,1)S(1)}, u32[]{:S(2)}, u32[]{:S(2)}) collective-permute-start(bf16[64,1024]{1,0:T(8,128)(2,1)S(1)} %reduce_sum.12), channel_id=1, source_target_pairs={{0,2},{2,0},{4,6},{6,4},{1,3},{3,1},{5,7},{7,5},{8,10},{10,8},{12,... | collective-permute-start | bytes 393224 | tf_op jit(solution)/shard_map/ppermute | solution.py:351
  155.3 4.9 %collective-permute-start.7 = (bf16[64,1024]{1,0:T(8,128)(2,1)S(1)}, bf16[64,1024]{1,0:T(8,128)(2,1)S(1)}, u32[]{:S(2)}, u32[]{:S(2)}) collective-permute-start(bf16[64,1024]{1,0:T(8,128)(2,1)S(1)} %reduce_sum.12), channel_id=1, source_target_pairs={{0,4},{2,6},{4,0},{6,2},{1,5},{3,7},{5,1},{7,3},{8,12},{10,14},{12... | collective-permute-start | bytes 393224 | tf_op jit(solution)/shard_map/ppermute | solution.py:351
  156.1 5.4 %collective-permute-start.8 = (bf16[64,1024]{1,0:T(8,128)(2,1)S(1)}, bf16[64,1024]{1,0:T(8,128)(2,1)S(1)}, u32[]{:S(2)}, u32[]{:S(2)}) collective-permute-start(bf16[64,1024]{1,0:T(8,128)(2,1)S(1)} %reduce_sum.12), channel_id=1, source_target_pairs={{0,6},{2,4},{4,2},{6,0},{1,7},{3,5},{5,3},{7,1},{8,14},{10,12},{12... | collective-permute-start | bytes 393224 | tf_op jit(solution)/shard_map/ppermute | solution.py:351
  156.5 50.9 %collective-permute-start = (bf16[16,32,16,128]{3,2,1,0:T(8,128)(2,1)}, bf16[16,32,16,128]{3,2,1,0:T(8,128)(2,1)}, u32[]{:S(2)}, u32[]{:S(2)}) collective-permute-start(bf16[16,32,16,128]{3,2,1,0:T(8,128)(2,1)} %copy-done.9), channel_id=1, source_target_pairs={{0,4},{4,0},{1,5},{5,1},{2,6},{6,2},{3,7},{7,3},{8,12},{12,8},{9,1... | collective-permute-start | bytes 6291464 | tf_op jit(solution)/shard_map/ppermute | solution.py:375
  195.5 32.4 %copy-start.3 = (bf16[16,64,512]{2,1,0:T(8,128)(2,1)}, bf16[16,64,512]{2,1,0:T(8,128)(2,1)S(1)}, u32[]{:S(2)}) copy-start(bf16[16,64,512]{2,1,0:T(8,128)(2,1)S(1)} %all_to_all.35) | copy-start | bytes 3145732
  195.5 5.6 %copy-start.7 = (f32[512,512]{1,0:T(8,128)S(1)}, f32[512,512]{1,0:T(8,128)}, u32[]{:S(2)}) copy-start(f32[512,512]{1,0:T(8,128)} %param.8) | copy-start | bytes 3145732
  196.7 5.9 %copy-start.6 = (f32[512,512]{1,0:T(8,128)S(1)}, f32[512,512]{1,0:T(8,128)}, u32[]{:S(2)}) copy-start(f32[512,512]{1,0:T(8,128)} %param.9) | copy-start | bytes 3145732
  196.7 17.7 %all-to-all-start.4 = ((bf16[16,64,512]{2,1,0:T(8,128)(2,1)}), bf16[16,64,512]{2,1,0:T(8,128)(2,1)}, u32[]{:S(2)}, u32[]{:S(2)}) async-start(bf16[16,64,512]{2,1,0:T(8,128)(2,1)} %broadcast_in_dim.4), calls=%async_computation.4 | async-start | bytes 2097152 | tf_op jit(solution)/shard_map/all_to_all | solution.py:355
  214.3 41.4 %collective-permute-start.1 = (bf16[16,32,16,128]{3,2,1,0:T(8,128)(2,1)}, bf16[16,32,16,128]{3,2,1,0:T(8,128)(2,1)}, u32[]{:S(2)}, u32[]{:S(2)}) collective-permute-start(bf16[16,32,16,128]{3,2,1,0:T(8,128)(2,1)} %get-tuple-element.21), channel_id=1, source_target_pairs={{0,4},{4,0},{1,5},{5,1},{2,6},{6,2},{3,7},{7,3},{8,12},{12,8},{9,1... | collective-permute-start | bytes 6291464 | tf_op jit(solution)/shard_map/ppermute | solution.py:411
  214.4 27.6 %all-to-all-start.6 = ((bf16[16,32,16,128]{3,2,1,0:T(8,128)(2,1)}), bf16[16,32,16,128]{3,2,1,0:T(8,128)(2,1)S(1)}, u32[]{:S(2)}, u32[]{:S(2)}) async-start(bf16[16,32,16,128]{3,2,1,0:T(8,128)(2,1)} %get-tuple-element.28), calls=%async_computation.6 | async-start | bytes 4194304 | tf_op jit(solution)/shard_map/all_to_all | solution.py:355
  220.9 55.0 %collective-permute-start.9 = (bf16[1024,512]{1,0:T(8,128)(2,1)}, bf16[1024,512]{1,0:T(8,128)(2,1)}, u32[]{:S(2)}, u32[]{:S(2)}) collective-permute-start(bf16[1024,512]{1,0:T(8,128)(2,1)} %bitcast.21.own), channel_id=1, source_target_pairs={{0,1},{1,0},{2,3},{3,2},{4,5},{5,4},{6,7},{7,6},{8,9},{9,8},{10,11... | collective-permute-start | bytes 3145736 | tf_op jit(solution)/shard_map/ppermute | solution.py:347
  227.9 67.8 %collective-permute-start.11 = (bf16[1024,512]{1,0:T(8,128)(2,1)S(1)}, bf16[1024,512]{1,0:T(8,128)(2,1)}, u32[]{:S(2)}, u32[]{:S(2)}) collective-permute-start(bf16[1024,512]{1,0:T(8,128)(2,1)S(1)} %bitcast.82), channel_id=1, source_target_pairs={{0,1},{1,0},{2,3},{3,2},{4,5},{5,4},{6,7},{7,6},{8,9},{9,8},{10,11... | collective-permute-start | bytes 3145736 | tf_op jit(solution)/shard_map/ppermute | solution.py:347
  242.0 13.8 %copy-start.5 = (bf16[16,32,16,128]{3,2,1,0:T(8,128)(2,1)}, bf16[16,32,16,128]{3,2,1,0:T(8,128)(2,1)S(1)}, u32[]{:S(2)}) copy-start(bf16[16,32,16,128]{3,2,1,0:T(8,128)(2,1)S(1)} %all-to-all-done.6.t) | copy-start | bytes 6291460
  255.8 107.1 %all-to-all-start.2 = ((bf16[16,32,16,128]{3,2,1,0:T(8,128)(2,1)}), bf16[16,32,16,128]{3,2,1,0:T(8,128)(2,1)S(1)}, u32[]{:S(2)}, u32[]{:S(2)}) async-start(bf16[16,32,16,128]{3,2,1,0:T(8,128)(2,1)} %collective-permute-done.1), calls=%async_computation.2 | async-start | bytes 4194304 | tf_op jit(solution)/shard_map/all_to_all | solution.py:355
  288.1 21.0 %copy-start.12 = (f32[512]{0:T(512)S(1)}, f32[512]{0:T(512)}, u32[]{:S(2)}) copy-start(f32[512]{0:T(512)} %param.13) | copy-start | bytes 6148
  288.1 67.0 %collective-permute-start.10 = (bf16[2,2048,128]{2,1,0:T(8,128)(2,1)}, bf16[2,2048,128]{2,1,0:T(8,128)(2,1)}, u32[]{:S(2)}, u32[]{:S(2)}) collective-permute-start(bf16[2,2048,128]{2,1,0:T(8,128)(2,1)} %get-tuple-element.23), channel_id=1, source_target_pairs={{0,1},{1,0},{2,3},{3,2},{4,5},{5,4},{6,7},{7,6},{8,9},{9,8},{10,11... | collective-permute-start | bytes 3145736 | tf_op jit(solution)/shard_map/ppermute | solution.py:347
  306.0 49.1 %collective-permute-start.13 = (bf16[2,1536,128]{2,1,0:T(8,128)(2,1)}, bf16[2,1536,128]{2,1,0:T(8,128)(2,1)S(1)}, u32[]{:S(2)}, u32[]{:S(2)}) collective-permute-start(bf16[2,1536,128]{2,1,0:T(8,128)(2,1)} %get-tuple-element.25), channel_id=1, source_target_pairs={{0,2},{1,3},{2,0},{3,1},{4,6},{5,7},{6,4},{7,5},{8,10},{9,11},{10,... | collective-permute-start | bytes 2359304 | tf_op jit(solution)/shard_map/ppermute | solution.py:347
  308.0 47.1 %collective-permute-start.15 = (bf16[2,1536,128]{2,1,0:T(8,128)(2,1)}, bf16[2,1536,128]{2,1,0:T(8,128)(2,1)}, u32[]{:S(2)}, u32[]{:S(2)}) collective-permute-start(bf16[2,1536,128]{2,1,0:T(8,128)(2,1)} %get-tuple-element.27), channel_id=1, source_target_pairs={{0,3},{1,2},{2,1},{3,0},{4,7},{5,6},{6,5},{7,4},{8,11},{9,10},{10,... | collective-permute-start | bytes 2359304 | tf_op jit(solution)/shard_map/ppermute | solution.py:347
  318.0 31.3 %collective-permute-start.12 = (bf16[2,512,128]{2,1,0:T(8,128)(2,1)}, bf16[2,512,128]{2,1,0:T(8,128)(2,1)S(1)}, u32[]{:S(2)}, u32[]{:S(2)}) collective-permute-start(bf16[2,512,128]{2,1,0:T(8,128)(2,1)} %get-tuple-element.24), channel_id=1, source_target_pairs={{0,2},{1,3},{2,0},{3,1},{4,6},{5,7},{6,4},{7,5},{8,10},{9,11},{10,... | collective-permute-start | bytes 786440 | tf_op jit(solution)/shard_map/ppermute | solution.py:347
  320.0 35.1 %collective-permute-start.14 = (bf16[2,512,128]{2,1,0:T(8,128)(2,1)}, bf16[2,512,128]{2,1,0:T(8,128)(2,1)S(1)}, u32[]{:S(2)}, u32[]{:S(2)}) collective-permute-start(bf16[2,512,128]{2,1,0:T(8,128)(2,1)} %get-tuple-element.26), channel_id=1, source_target_pairs={{0,3},{1,2},{2,1},{3,0},{4,7},{5,6},{6,5},{7,4},{8,11},{9,10},{10,... | collective-permute-start | bytes 786440 | tf_op jit(solution)/shard_map/ppermute | solution.py:347
  349.3 5.8 %copy-start.10 = (bf16[2,512,128]{2,1,0:T(8,128)(2,1)}, bf16[2,512,128]{2,1,0:T(8,128)(2,1)S(1)}, u32[]{:S(2)}) copy-start(bf16[2,512,128]{2,1,0:T(8,128)(2,1)S(1)} %collective-permute-done.12) | copy-start | bytes 786436
  355.1 0.7 copy-start.11
  355.1 1.0 copy-start.8
  362.9 1.3 copy-start.4
where the time goes:
time: 374 us; the launch traced here: 371 us
  Pallas kernels  133 us (36%)
  waiting for transfers between devices  124 us (33%)
  starting transfers between devices  65.2 us (17%)
  blocking collectives  17.5 us (5%)
  local copies, waits for them, and re-layouts  12.8 us (3%)
  other arithmetic  10.3 us (3%)
  matrix products  6.74 us (2%)
    all_to_all x6, waiting for transfers between devices, to_owner(): return lax.all_to_all(v, axes, split_axis=0, concat_axis=0, tiled=True)  64.2 us
    ppermute x11, waiting for transfers between devices, swap(): return lax.ppermute(v, ('zh', 'c'), [(d, d ^ s) for d in range(4)])  41.5 us
    all_to_all x6, starting transfers between devices, to_owner(): return lax.all_to_all(v, axes, split_axis=0, concat_axis=0, tiled=True)  35 us
    pallas_call x3, Pallas kernels, second(): call(functools.partial(second_body, far), (shape((2, steps * 512, 128)),)...  28.7 us
    ppermute x11, starting transfers between devices, swap(): return lax.ppermute(v, ('zh', 'c'), [(d, d ^ s) for d in range(4)])  26.6 us
    pallas_call x2, Pallas kernels, project(): call(project_body, shape((1024, 1024), dtype), (2,), [pl.BlockSpec((512,...  21.5 us
    all_to_all x1, blocking collectives, to_owner(): return lax.all_to_all(v, axes, split_axis=0, concat_axis=0, tiled=True)  17.5 us
    pallas_call x1, Pallas kernels, base(): call(base_body, shape((2, 16, 512, 128), F32), (16,), [pl.BlockSpec((2, 1...  14.5 us
  transfers between devices with their start and end apart: 22, of which 12 were waited for; matrix products, arithmetic and copies ran while one was open for 7% of the time, Pallas kernels for 30%

commit v1 on v0

--- a/solution.py
+++ b/solution.py
@@ -70,11 +70,10 @@
     )(me, g)
 
 
-def deal_body(me, *refs):
-    gs, t_out, scr = refs[:4], refs[4], refs[5]
-    for sub, g in enumerate(gs):
+def deal_body(me, g, t_out, scr):
+    for sub in range(4):
         for i in range(16):
-            scr[pl.ds(i * 40, 32), :] = g[i].astype(F32)
+            scr[pl.ds(i * 40, 32), :] = g[i, sub * 32 : sub * 32 + 32, :].astype(F32)
         for kc in range(32):
             t_out[sub, kc] = scr[pl.ds(kc, 16, stride=40), :].astype(BF16)
 
@@ -83,21 +82,17 @@
     return 1 - me[1] if other else me[1]
 
 
-def deal(me, g, other):
-    def piece(sub):
-        at = lambda t, me: (0, (t * 4 + sub) * 2 + side_of(me, other), 0)
-        return pl.BlockSpec((16, 32, 128), at)
-
+def deal(me, g):
     return call(
         deal_body,
-        shape((16, 32, 16, 128)),
-        (4,),
-        [piece(sub) for sub in range(4)],
+        shape((32, 32, 16, 128)),
+        (8,),
+        [pl.BlockSpec((16, 128, 128), lambda t, me: (0, t, 0))],
         pl.BlockSpec((4, 32, 16, 128), lambda t, me: (t, 0, 0, 0)),
         [pltpu.VMEM((640, 128), F32)],
         1 << 24,
-        4 << 20,
-    )(me, g, g, g, g)
+        8 << 20,
+    )(me, g)
 
 
 def flat_body(me, l, la, scr):
@@ -257,8 +252,8 @@
     for j in range(4):
         halves = []
         for kc in (2 * j, 2 * j + 1):
-            first = jnp.where(low, own[:, kc], oth[:, kc])
-            last = jnp.where(low, oth[:, kc], own[:, kc])
+            first = jnp.where(low, own[:, 0, kc], oth[:, kc])
+            last = jnp.where(low, oth[:, kc], own[:, 0, kc])
             halves.append(jnp.stack([first, last], axis=1).reshape(512, 128))
         both = jnp.concatenate(halves, axis=1)
         y = jnp.dot(ham[...], both, preferred_element_type=F32).astype(BF16)
@@ -274,7 +269,11 @@
         mix_body,
         (shape((16, 32, 16, 128)),) * 2,
         (4,),
-        [block, block, whole((512, 512))],
+        [
+            pl.BlockSpec((16, 1, 8, 16, 128), lambda t, me: (0, me[1], t, 0, 0)),
+            block,
+            whole((512, 512)),
+        ],
         (block, block),
         [],
         1 << 31,
@@ -370,11 +369,10 @@
     w1 = swap(e1, 1)
     e = (e0, e1, e2, e3)
     w = [v.reshape(2, rows * 128, cols) for v in (e0, w1, w2, w3)]
-    dealt_oth = deal(me, g, True)
-    part_oth = to_owner(dealt_oth, plane)
+    dealt = deal(me, g)
+    part = to_owner(dealt, plane).reshape(16, 2, 32, 16, 128)
+    part_oth = lax.dynamic_index_in_dim(part, 1 - side, 1, keepdims=False)
     part_oth = lax.ppermute(part_oth, "zl", [(0, 1), (1, 0)])
-    dealt_own = deal(me, g, False)
-    part_own = to_owner(dealt_own, plane)
 
     hamil = 0.5 * (core_ham + core_ham.T) + field[0] * (0.5 * (dipole + dipole.T))
     ham = hamil.astype(BF16)
@@ -407,7 +405,7 @@
     near = to_owner(jnp.broadcast_to(near[None], (16, 64, 512)), plane).reshape(1024, 512)
     near_oth = swap(near, 1)
 
-    mixed_own, mixed_oth = mix(me, part_own, part_oth, ham)
+    mixed_own, mixed_oth = mix(me, part, part_oth, ham)
     mixed_oth = lax.ppermute(mixed_oth, "zl", [(0, 1), (1, 0)])
     term_own = to_owner(mixed_own, plane)
     term_oth = to_owner(mixed_oth, plane)

time: 374 us -> 401 us (1.072)
  waiting for transfers between devices: 124 us -> 144 us
  blocking collectives: 17.5 us -> 24 us
    all_to_all x6 -> x5, waiting for transfers between devices: 64.2 us -> 90.3 us  [to_owner(): return lax.all_to_all(v, axes, split_axis=0, concat_axis=0, tiled=True)]
    ppermute x1, waiting for transfers between devices: 13.8 us -> 4.69 us  [per_device(): mixed_oth = lax.ppermute(mixed_oth, 'zl', [(0, 1), (1, 0)])]
    all_to_all x6 -> x5, starting transfers between devices: 35 us -> 43.6 us  [to_owner(): return lax.all_to_all(v, axes, split_axis=0, concat_axis=0, tiled=True)]
    ppermute x1, waiting for transfers between devices: 0.01 us -> 7.24 us  [per_device(): part_oth = lax.ppermute(part_oth, 'zl', [(0, 1), (1, 0)])]
    all_to_all x1, blocking collectives: 17.5 us -> 24 us  [to_owner(): return lax.all_to_all(v, axes, split_axis=0, concat_axis=0, tiled=True)]
    ppermute x11, starting transfers between devices: 26.6 us -> 20.4 us  [swap(): return lax.ppermute(v, ('zh', 'c'), [(d, d ^ s) for d in range(4)])]
    ppermute x3, waiting for transfers between devices: 4.7 us -> 0.01 us  [across(): return lax.ppermute(v, ('zl', 'zh'), [(d, d ^ s) for d in range(4)])]
    pallas_call x3 -> x2, Pallas kernels: 16.9 us -> 15 us  [the longest x1 8.06 us: deal(): call(deal_body, shape((32, 32, 16, 128)), (8,), [pl.BlockSpec((16, 128, 1...]
  transfers between devices with their start and end apart: 22 -> 21, of which waited for: 12 -> 9; matrix products, arithmetic and copies ran while one was open for 7% -> 6% of each run, Pallas kernels for 30% -> 27%
where the time goes in v1:
time: 401 us; the launch traced here: 399 us
  waiting for transfers between devices  144 us (36%)
  Pallas kernels  131 us (33%)
  starting transfers between devices  67.4 us (17%)
  blocking collectives  24 us (6%)
  local copies, waits for them, and re-layouts  14.9 us (4%)
  other arithmetic  9.57 us (2%)
  matrix products  6.76 us (2%)
    all_to_all x5, waiting for transfers between devices, to_owner(): return lax.all_to_all(v, axes, split_axis=0, concat_axis=0, tiled=True)  90.3 us
    all_to_all x5, starting transfers between devices, to_owner(): return lax.all_to_all(v, axes, split_axis=0, concat_axis=0, tiled=True)  43.6 us
    ppermute x11, waiting for transfers between devices, swap(): return lax.ppermute(v, ('zh', 'c'), [(d, d ^ s) for d in range(4)])  41.5 us
    pallas_call x3, Pallas kernels, second(): call(functools.partial(second_body, far), (shape((2, steps * 512, 128)),)...  28.6 us
    all_to_all x1, blocking collectives, to_owner(): return lax.all_to_all(v, axes, split_axis=0, concat_axis=0, tiled=True)  24 us
    pallas_call x2, Pallas kernels, project(): call(project_body, shape((1024, 1024), dtype), (2,), [pl.BlockSpec((512,...  21.5 us
    ppermute x11, starting transfers between devices, swap(): return lax.ppermute(v, ('zh', 'c'), [(d, d ^ s) for d in range(4)])  20.4 us
    pallas_call x1, Pallas kernels, base(): call(base_body, shape((2, 16, 512, 128), F32), (16,), [pl.BlockSpec((2, 1...  14.5 us
  transfers between devices with their start and end apart: 21, of which 9 were waited for; matrix products, arithmetic and copies ran while one was open for 6% of the time, Pallas kernels for 27%

profile of v1, /device:TPU:1, one launch (start us, length us, event | category | flops | bytes accessed | tf_op | source)
XLA Modules:
  0.0 398.6 jit_solution(4434293293723059007)
XLA Ops:
  0.6 5.0 %shard_map.73 = (bf16[2,16,128,128]{3,2,1,0:T(8,128)(2,1)}, bf16[2,16,128,128]{3,2,1,0:T(8,128)(2,1)}) custom-call(s32[2]{0:T(128)} %pad_add_fusion.me, bf16[16,1024,128]{2,1,0:T(8,128)(2,1)} %bitcast.55), custom_call_target="tpu_custom_call" | custom-call | flops 16777216 | bytes 4194304 | tf_op jit(solution)/shard_map/pallas_call | solution.py:61
  5.6 1.4 collective-permute-start.2
  7.0 5.0 %shard_map.74 = (bf16[2,16,128,128]{3,2,1,0:T(8,128)(2,1)}, bf16[2,16,128,128]{3,2,1,0:T(8,128)(2,1)}) custom-call(s32[2]{0:T(128)} %pad_add_fusion.me, bf16[16,1024,128]{2,1,0:T(8,128)(2,1)} %bitcast.56), custom_call_target="tpu_custom_call" | custom-call | flops 16777216 | bytes 4194304 | tf_op jit(solution)/shard_map/pallas_call | solution.py:61
  12.0 3.7 collective-permute-start.3
  15.7 0.7 slice.7
  16.4 14.4 %shard_map.78.la = bf16[2048,2048]{1,0:T(8,128)(2,1)} custom-call(s32[2]{0:T(128)} %pad_add_fusion.me, bf16[2048,16,128]{2,1,0:T(8,128)(2,1)} %l.1), custom_call_target="tpu_custom_call" | custom-call | flops 16777216 | bytes 16777216 | tf_op jit(solution)/shard_map/pallas_call | solution.py:107
  30.7 0.8 constant_dynamic-slice_fusion.2
  32.2 6.8 %fusion.2.z = f32[2048,2]{1,0:T(8,128)} fusion(bf16[2048,16,128]{2,1,0:T(8,128)(2,1)} %l.1, bf16[2,16,128]{2,1,0:T(8,128)(2,1)S(1)} %constant_dynamic-slice_fusion.2), kind=kOutput, calls=%fused_computation.3 | convolution fusion | flops 16777216 | bytes 8413184 | tf_op jit(solution)/shard_map/dot_general | solution.py:381
  39.4 22.5 %collective-permute-done.4 = bf16[2,16,128,128]{3,2,1,0:T(8,128)(2,1)S(1)} collective-permute-done((bf16[2,16,128,128]{3,2,1,0:T(8,128)(2,1)}, bf16[2,16,128,128]{3,2,1,0:T(8,128)(2,1)S(1)}, u32[]{:S(2)}, u32[]{:S(2)}) %collective-permute-start.4) | collective-permute-done | bytes 1048608 | tf_op jit(solution)/shard_map/ppermute | solution.py:346
  61.9 1.0 copy-done.2
  62.9 10.6 %shard_map.81 = bf16[1024,1024]{1,0:T(8,128)(2,1)} custom-call(s32[2]{0:T(128)} %pad_add_fusion.me, bf16[2048,2048]{1,0:T(8,128)(2,1)} %shard_map.78.la, bf16[2,2048,128]{2,1,0:T(8,128)(2,1)} %bitcast.58, bf16[2,2048,128]{2,1,0:T(8,128)(2,1)} %bitcast.63, bf16[2,2048,128]{2,1,0:T(8,128)(2,1)} %bitcast.68, bf16[2,2048,128]{2,1,0:T(8,128)(2,1)} %bitcast.73, ...), custom_call_target="tpu_custom_call" | custom-call | flops 4294967296 | bytes 10485760 | tf_op jit(solution)/shard_map/pallas_call | solution.py:193
  73.8 10.9 %shard_map.80 = f32[1024,1024]{1,0:T(8,128)} custom-call(s32[2]{0:T(128)} %pad_add_fusion.me, bf16[2048,2048]{1,0:T(8,128)(2,1)} %shard_map.78.la, bf16[2,2048,128]{2,1,0:T(8,128)(2,1)} %bitcast.59, bf16[2,2048,128]{2,1,0:T(8,128)(2,1)} %bitcast.64, bf16[2,2048,128]{2,1,0:T(8,128)(2,1)} %bitcast.69, bf16[2,2048,128]{2,1,0:T(8,128)(2,1)} %bitcast.74, ...), custom_call_target="tpu_custom_call" | custom-call | flops 4294967296 | bytes 10485760 | tf_op jit(solution)/shard_map/pallas_call | solution.py:193
  84.7 4.3 %add_convert_fusion = bf16[1024,1024]{1,0:T(8,128)(2,1)} fusion(f32[1024,1024]{1,0:T(8,128)} %shard_map.80, bf16[1024,1024]{1,0:T(8,128)(2,1)S(1)} %collective-permute-done.5), kind=kLoop, calls=%fused_computation.2 | loop fusion | flops 3145728 | bytes 8388608 | tf_op jit(solution)/shard_map/convert_element_type | solution.py:394
  89.1 6.8 %all-to-all-start.2 = ((bf16[16,64,1024]{2,1,0:T(8,128)(2,1)}), bf16[16,64,1024]{2,1,0:T(8,128)(2,1)S(1)}, u32[]{:S(2)}, u32[]{:S(2)}) async-start(bf16[16,64,1024]{2,1,0:T(8,128)(2,1)} %bitcast.81), calls=%async_computation.2 | async-start | bytes 4194304 | tf_op jit(solution)/shard_map/all_to_all | solution.py:354
  95.8 8.1 %shard_map.76 = bf16[32,32,16,128]{3,2,1,0:T(8,128)(2,1)} custom-call(s32[2]{0:T(128)} %pad_add_fusion.me, bf16[16,1024,128]{2,1,0:T(8,128)(2,1)} %bitcast.57), custom_call_target="tpu_custom_call" | custom-call | flops 16777216 | bytes 8388608 | tf_op jit(solution)/shard_map/pallas_call | solution.py:86
  103.9 21.1 %all-to-all-done.2 = bf16[16,64,1024]{2,1,0:T(8,128)(2,1)S(1)} async-done(((bf16[16,64,1024]{2,1,0:T(8,128)(2,1)}), bf16[16,64,1024]{2,1,0:T(8,128)(2,1)S(1)}, u32[]{:S(2)}, u32[]{:S(2)}) %all-to-all-start.2) | async-done | bytes 2097184 | tf_op jit(solution)/shard_map/all_to_all | solution.py:354
  124.9 5.5 %all-to-all-start = ((bf16[32,32,16,128]{3,2,1,0:T(8,128)(2,1)}), bf16[32,32,16,128]{3,2,1,0:T(8,128)(2,1)}, u32[]{:S(2)}, u32[]{:S(2)}) async-start(bf16[32,32,16,128]{3,2,1,0:T(8,128)(2,1)} %shard_map.76), calls=%async_computation | async-start | bytes 8388608 | tf_op jit(solution)/shard_map/all_to_all | solution.py:354
  130.8 2.3 collective-permute-start.6
  133.1 0.8 collective-permute-start.7
  134.2 48.1 %all-to-all-done = bf16[32,32,16,128]{3,2,1,0:T(8,128)(2,1)} async-done(((bf16[32,32,16,128]{3,2,1,0:T(8,128)(2,1)}), bf16[32,32,16,128]{3,2,1,0:T(8,128)(2,1)}, u32[]{:S(2)}, u32[]{:S(2)}) %all-to-all-start) | async-done | bytes 4194336 | tf_op jit(solution)/shard_map/all_to_all | solution.py:354
  182.3 3.4 dynamic-slice_bitcast_fusion
  186.0 24.0 %all_to_all.30 = bf16[16,64,512]{2,1,0:T(8,128)(2,1)S(1)} all-to-all(bf16[16,64,512]{2,1,0:T(8,128)(2,1)S(1)} %broadcast_in_dim.5), channel_id=1, replica_groups=mesh['x'=4,'y'=4,'zl'=2,'zh'=2,'c'=2] {'x','y'}, dimensions={0} | all-to-all | bytes 2097152 | tf_op jit(solution)/shard_map/all_to_all | solution.py:354
  210.1 1.2 broadcast_in_dim.4
  211.3 4.4 %all-to-all-start.3 = ((bf16[16,64,512]{2,1,0:T(8,128)(2,1)}), bf16[16,64,512]{2,1,0:T(8,128)(2,1)}, u32[]{:S(2)}, u32[]{:S(2)}) async-start(bf16[16,64,512]{2,1,0:T(8,128)(2,1)} %broadcast_in_dim.4), calls=%async_computation.3 | async-start | bytes 2097152 | tf_op jit(solution)/shard_map/all_to_all | solution.py:354
  215.7 1.3 copy.17
  217.0 1.3 copy.18
  219.0 2.9 fusion.7.ham
  221.8 7.2 %collective-permute-done.oth = bf16[16,32,16,128]{3,2,1,0:T(8,128)(2,1)} collective-permute-done((bf16[16,32,16,128]{3,2,1,0:T(8,128)(2,1)}, bf16[16,32,16,128]{3,2,1,0:T(8,128)(2,1)}, u32[]{:S(2)}, u32[]{:S(2)}) %collective-permute-start) | collective-permute-done | bytes 2097184 | tf_op jit(solution)/shard_map/ppermute | solution.py:375
  229.1 6.9 %shard_map.77 = (bf16[16,32,16,128]{3,2,1,0:T(8,128)(2,1)}, bf16[16,32,16,128]{3,2,1,0:T(8,128)(2,1)}) custom-call(s32[2]{0:T(128)} %pad_add_fusion.me, bf16[16,2,32,16,128]{4,3,2,1,0:T(8,128)(2,1)} %bitcast.11.own, bf16[16,32,16,128]{3,2,1,0:T(8,128)(2,1)} %collective-permute-done.oth, bf16[512,512]{1,0:T(8,128)(2,1)} %fusion.7.ham), custom_call_target="tpu_custom_call" | custom-call | flops 2147483648 | bytes 8388608 | tf_op jit(solution)/shard_map/pallas_call | solution.py:268
  236.0 12.8 %all-to-all-start.5 = ((bf16[16,32,16,128]{3,2,1,0:T(8,128)(2,1)}), bf16[16,32,16,128]{3,2,1,0:T(8,128)(2,1)S(1)}, u32[]{:S(2)}, u32[]{:S(2)}) async-start(bf16[16,32,16,128]{3,2,1,0:T(8,128)(2,1)} %get-tuple-element.28), calls=%async_computation.5 | async-start | bytes 4194304 | tf_op jit(solution)/shard_map/all_to_all | solution.py:354
  248.8 3.9 collective-permute-start.9
  252.8 21.1 %all-to-all-done.5.t = bf16[16,32,16,128]{3,2,1,0:T(8,128)(2,1)S(1)} async-done(((bf16[16,32,16,128]{3,2,1,0:T(8,128)(2,1)}), bf16[16,32,16,128]{3,2,1,0:T(8,128)(2,1)S(1)}, u32[]{:S(2)}, u32[]{:S(2)}) %all-to-all-start.5) | async-done | bytes 2097184 | tf_op jit(solution)/shard_map/all_to_all | solution.py:354
  273.9 4.7 %collective-permute-done.1 = bf16[16,32,16,128]{3,2,1,0:T(8,128)(2,1)} collective-permute-done((bf16[16,32,16,128]{3,2,1,0:T(8,128)(2,1)}, bf16[16,32,16,128]{3,2,1,0:T(8,128)(2,1)}, u32[]{:S(2)}, u32[]{:S(2)}) %collective-permute-start.1) | collective-permute-done | bytes 2097184 | tf_op jit(solution)/shard_map/ppermute | solution.py:409
  278.6 14.2 %all-to-all-start.1 = ((bf16[16,32,16,128]{3,2,1,0:T(8,128)(2,1)}), bf16[16,32,16,128]{3,2,1,0:T(8,128)(2,1)S(1)}, u32[]{:S(2)}, u32[]{:S(2)}) async-start(bf16[16,32,16,128]{3,2,1,0:T(8,128)(2,1)} %collective-permute-done.1), calls=%async_computation.1 | async-start | bytes 4194304 | tf_op jit(solution)/shard_map/all_to_all | solution.py:354
  292.8 13.9 %shard_map.79.lt = bf16[2048,2048]{1,0:T(8,128)(2,1)} custom-call(s32[2]{0:T(128)} %pad_add_fusion.me, bf16[2048,2048]{1,0:T(8,128)(2,1)} %shard_map.78.la), custom_call_target="tpu_custom_call" | custom-call | flops 67108864 | bytes 16777216 | tf_op jit(solution)/shard_map/pallas_call | solution.py:125
  306.7 12.2 %shard_map.82 = (bf16[2,2048,128]{2,1,0:T(8,128)(2,1)}, bf16[2,2048,128]{2,1,0:T(8,128)(2,1)}) custom-call(s32[2]{0:T(128)} %pad_add_fusion.me, bf16[2048,2048]{1,0:T(8,128)(2,1)} %shard_map.79.lt, bf16[1024,512]{1,0:T(8,128)(2,1)} %bitcast.23.own, bf16[1024,512]{1,0:T(8,128)(2,1)} %collective-permute-done.9.oth, bf16[2,2048,128]{2,1,0:T(8,128)(2,1)} %bitcast.60, ...), custom_call_target="tpu_custom_call" | custom-call | flops 2147483648 | bytes 8388608 | tf_op jit(solution)/shard_map/pallas_call | solution.py:232
  318.9 4.4 %collective-permute-start.10 = (bf16[2,2048,128]{2,1,0:T(8,128)(2,1)}, bf16[2,2048,128]{2,1,0:T(8,128)(2,1)}, u32[]{:S(2)}, u32[]{:S(2)}) collective-permute-start(bf16[2,2048,128]{2,1,0:T(8,128)(2,1)} %get-tuple-element.23), channel_id=1, source_target_pairs={{0,1},{1,0},{2,3},{3,2},{4,5},{5,4},{6,7},{7,6},{8,9},{9,8},{10,11... | collective-permute-start | bytes 3145736 | tf_op jit(solution)/shard_map/ppermute | solution.py:346
  323.3 10.3 %shard_map.84 = (bf16[2,1536,128]{2,1,0:T(8,128)(2,1)}, bf16[2,1536,128]{2,1,0:T(8,128)(2,1)}) custom-call(s32[2]{0:T(128)} %pad_add_fusion.me, bf16[2048,2048]{1,0:T(8,128)(2,1)} %shard_map.79.lt, bf16[1024,512]{1,0:T(8,128)(2,1)} %bitcast.79, bf16[1024,512]{1,0:T(8,128)(2,1)} %collective-permute-done.11.oth, bf16[2,2048,128]{2,1,0:T(8,128)(2,1)} %bitcast.61, ...), custom_call_target="tpu_custom_call" | custom-call | flops 2147483648 | bytes 8388608 | tf_op jit(solution)/shard_map/pallas_call | solution.py:232
  333.6 3.1 collective-permute-start.15
  338.7 0.9 copy.19.dk
  339.6 6.1 %shard_map.83 = (bf16[2,512,128]{2,1,0:T(8,128)(2,1)}, bf16[2,512,128]{2,1,0:T(8,128)(2,1)}) custom-call(s32[2]{0:T(128)} %pad_add_fusion.me, bf16[2048,2048]{1,0:T(8,128)(2,1)} %shard_map.79.lt, bf16[1024,512]{1,0:T(8,128)(2,1)} %bitcast.80, bf16[1024,512]{1,0:T(8,128)(2,1)} %collective-permute-done.11.oth, bf16[2,2048,128]{2,1,0:T(8,128)(2,1)} %bitcast.62, ...), custom_call_target="tpu_custom_call" | custom-call | flops 2147483648 | bytes 8388608 | tf_op jit(solution)/shard_map/pallas_call | solution.py:232
  345.7 3.4 collective-permute-start.14
  349.7 14.5 %shard_map.75 = f32[2,16,512,128]{3,2,1,0:T(8,128)} custom-call(s32[2]{0:T(128)} %pad_add_fusion.me, bf16[2,16,128,128]{3,2,1,0:T(8,128)(2,1)} %get-tuple-element.17.e0, bf16[2,16,128,128]{3,2,1,0:T(8,128)(2,1)} %get-tuple-element.18.e1, bf16[2,16,128,128]{3,2,1,0:T(8,128)(2,1)} %get-tuple-element.19.e2, bf16[2,16,128,128]{3,2,1,0:T(8,128)(2,1)} %get-tuple-element.20.e3, ...), custom_call_target="tpu_custom_call" | custom-call | flops 2147483648 | bytes 12582912 | tf_op jit(solution)/shard_map/pallas_call | solution.py:152
  364.2 12.7 %collective-permute-done.12 = bf16[2,512,128]{2,1,0:T(8,128)(2,1)S(1)} collective-permute-done((bf16[2,512,128]{2,1,0:T(8,128)(2,1)}, bf16[2,512,128]{2,1,0:T(8,128)(2,1)S(1)}, u32[]{:S(2)}, u32[]{:S(2)}) %collective-permute-start.12) | collective-permute-done | bytes 262176 | tf_op jit(solution)/shard_map/ppermute | solution.py:346
  376.9 5.8 %collective-permute-done.14 = bf16[2,512,128]{2,1,0:T(8,128)(2,1)S(1)} collective-permute-done((bf16[2,512,128]{2,1,0:T(8,128)(2,1)}, bf16[2,512,128]{2,1,0:T(8,128)(2,1)S(1)}, u32[]{:S(2)}, u32[]{:S(2)}) %collective-permute-start.14) | collective-permute-done | bytes 262176 | tf_op jit(solution)/shard_map/ppermute | solution.py:346
  383.7 6.8 %shard_map.85.refs_0_ = bf16[16,16,2,32,128]{4,3,2,1,0:T(8,128)(2,1)} custom-call(s32[2]{0:T(128)} %pad_add_fusion.me, f32[2,16,16,2,16,128]{5,4,3,2,1,0:T(8,128)} %bitcast.53, bf16[16,32,16,128]{3,2,1,0:T(8,128)(2,1)} %copy-done.5, bf16[2,16,4,2,16,128]{5,4,3,2,1,0:T(8,128)(2,1)} %bitcast.82, bf16[2,16,4,2,16,128]{5,4,3,2,1,0:T(8,128)(2,1)} %bitcast.25.v1, ...), custom_call_target="tpu_custom_call" | custom-call | flops 16777216 | bytes 10485760 | tf_op jit(solution)/shard_map/pallas_call | solution.py:320
  390.5 1.4 copy-done.4
  391.9 6.8 %shard_map.86 = bf16[16,16,2,32,128]{4,3,2,1,0:T(8,128)(2,1)} custom-call(s32[2]{0:T(128)} %pad_add_fusion.me, f32[2,16,16,2,16,128]{5,4,3,2,1,0:T(8,128)} %bitcast.54, bf16[16,32,16,128]{3,2,1,0:T(8,128)(2,1)} %copy-done.4, bf16[2,16,4,2,16,128]{5,4,3,2,1,0:T(8,128)(2,1)} %bitcast.83, ...), custom_call_target="tpu_custom_call", output_to_operand_aliasing={{}: (9, {})} | custom-call | flops 16777216 | bytes 10485760 | tf_op jit(solution)/shard_map/pallas_call | solution.py:320
  (53 shorter events, 6.8 us)
Async XLA Ops:
  5.6 33.4 %collective-permute-start.2 = (bf16[2,16,128,128]{3,2,1,0:T(8,128)(2,1)}, bf16[2,16,128,128]{3,2,1,0:T(8,128)(2,1)S(1)}, u32[]{:S(2)}, u32[]{:S(2)}) collective-permute-start(bf16[2,16,128,128]{3,2,1,0:T(8,128)(2,1)} %get-tuple-element.18.e1), channel_id=1, source_target_pairs={{0,1},{1,0},{2,3},{3,2},{4,5},{5,4},{6,7},{7,6},{8,9},{9,8},{10,11... | collective-permute-start | bytes 3145736 | tf_op jit(solution)/shard_map/ppermute | solution.py:346
  12.0 27.4 %collective-permute-start.3 = (bf16[2,16,128,128]{3,2,1,0:T(8,128)(2,1)}, bf16[2,16,128,128]{3,2,1,0:T(8,128)(2,1)S(1)}, u32[]{:S(2)}, u32[]{:S(2)}) collective-permute-start(bf16[2,16,128,128]{3,2,1,0:T(8,128)(2,1)} %get-tuple-element.19.e2), channel_id=1, source_target_pairs={{0,2},{1,3},{2,0},{3,1},{4,6},{5,7},{6,4},{7,5},{8,10},{9,11},{10,... | collective-permute-start | bytes 3145736 | tf_op jit(solution)/shard_map/ppermute | solution.py:346
  15.7 46.2 %collective-permute-start.4 = (bf16[2,16,128,128]{3,2,1,0:T(8,128)(2,1)}, bf16[2,16,128,128]{3,2,1,0:T(8,128)(2,1)S(1)}, u32[]{:S(2)}, u32[]{:S(2)}) collective-permute-start(bf16[2,16,128,128]{3,2,1,0:T(8,128)(2,1)} %get-tuple-element.20.e3), channel_id=1, source_target_pairs={{0,3},{1,2},{2,1},{3,0},{4,7},{5,6},{6,5},{7,4},{8,11},{9,10},{10,... | collective-permute-start | bytes 3145736 | tf_op jit(solution)/shard_map/ppermute | solution.py:346
  38.9 23.0 %copy-start = (bf16[2,16,128,128]{3,2,1,0:T(8,128)(2,1)}, bf16[2,16,128,128]{3,2,1,0:T(8,128)(2,1)S(1)}, u32[]{:S(2)}) copy-start(bf16[2,16,128,128]{3,2,1,0:T(8,128)(2,1)S(1)} %collective-permute-done.2) | copy-start | bytes 3145732
  39.4 22.5 %copy-start.1 = (bf16[2,16,128,128]{3,2,1,0:T(8,128)(2,1)}, bf16[2,16,128,128]{3,2,1,0:T(8,128)(2,1)S(1)}, u32[]{:S(2)}) copy-start(bf16[2,16,128,128]{3,2,1,0:T(8,128)(2,1)S(1)} %collective-permute-done.3) | copy-start | bytes 3145732
  61.9 1.0 copy-start.2
  73.4 11.3 %collective-permute-start.5 = (bf16[1024,1024]{1,0:T(8,128)(2,1)}, bf16[1024,1024]{1,0:T(8,128)(2,1)S(1)}, u32[]{:S(2)}, u32[]{:S(2)}) collective-permute-start(bf16[1024,1024]{1,0:T(8,128)(2,1)} %shard_map.81), channel_id=1, source_target_pairs={{0,1},{1,0},{2,3},{3,2},{4,5},{5,4},{6,7},{7,6},{8,9},{9,8},{10,11... | collective-permute-start | bytes 6291464 | tf_op jit(solution)/shard_map/ppermute | solution.py:346
  89.1 35.9 %all-to-all-start.2 = ((bf16[16,64,1024]{2,1,0:T(8,128)(2,1)}), bf16[16,64,1024]{2,1,0:T(8,128)(2,1)S(1)}, u32[]{:S(2)}, u32[]{:S(2)}) async-start(bf16[16,64,1024]{2,1,0:T(8,128)(2,1)} %bitcast.81), calls=%async_computation.2 | async-start | bytes 4194304 | tf_op jit(solution)/shard_map/all_to_all | solution.py:354
  124.9 57.4 %all-to-all-start = ((bf16[32,32,16,128]{3,2,1,0:T(8,128)(2,1)}), bf16[32,32,16,128]{3,2,1,0:T(8,128)(2,1)}, u32[]{:S(2)}, u32[]{:S(2)}) async-start(bf16[32,32,16,128]{3,2,1,0:T(8,128)(2,1)} %shard_map.76), calls=%async_computation | async-start | bytes 8388608 | tf_op jit(solution)/shard_map/all_to_all | solution.py:354
  130.8 55.0 %collective-permute-start.6 = (bf16[64,1024]{1,0:T(8,128)(2,1)S(1)}, bf16[64,1024]{1,0:T(8,128)(2,1)S(1)}, u32[]{:S(2)}, u32[]{:S(2)}) collective-permute-start(bf16[64,1024]{1,0:T(8,128)(2,1)S(1)} %reduce_sum.12), channel_id=1, source_target_pairs={{0,2},{2,0},{4,6},{6,4},{1,3},{3,1},{5,7},{7,5},{8,10},{10,8},{12,... | collective-permute-start | bytes 393224 | tf_op jit(solution)/shard_map/ppermute | solution.py:350
  133.1 52.7 %collective-permute-start.7 = (bf16[64,1024]{1,0:T(8,128)(2,1)S(1)}, bf16[64,1024]{1,0:T(8,128)(2,1)S(1)}, u32[]{:S(2)}, u32[]{:S(2)}) collective-permute-start(bf16[64,1024]{1,0:T(8,128)(2,1)S(1)} %reduce_sum.12), channel_id=1, source_target_pairs={{0,4},{2,6},{4,0},{6,2},{1,5},{3,7},{5,1},{7,3},{8,12},{10,14},{12... | collective-permute-start | bytes 393224 | tf_op jit(solution)/shard_map/ppermute | solution.py:350
  133.9 51.9 %collective-permute-start.8 = (bf16[64,1024]{1,0:T(8,128)(2,1)S(1)}, bf16[64,1024]{1,0:T(8,128)(2,1)S(1)}, u32[]{:S(2)}, u32[]{:S(2)}) collective-permute-start(bf16[64,1024]{1,0:T(8,128)(2,1)S(1)} %reduce_sum.12), channel_id=1, source_target_pairs={{0,6},{2,4},{4,2},{6,0},{1,7},{3,5},{5,3},{7,1},{8,14},{10,12},{12... | collective-permute-start | bytes 393224 | tf_op jit(solution)/shard_map/ppermute | solution.py:350
  185.7 30.0 %copy-start.7 = (f32[512,512]{1,0:T(8,128)S(1)}, f32[512,512]{1,0:T(8,128)}, u32[]{:S(2)}) copy-start(f32[512,512]{1,0:T(8,128)} %param.8) | copy-start | bytes 3145732
  185.7 43.4 %collective-permute-start = (bf16[16,32,16,128]{3,2,1,0:T(8,128)(2,1)}, bf16[16,32,16,128]{3,2,1,0:T(8,128)(2,1)}, u32[]{:S(2)}, u32[]{:S(2)}) collective-permute-start(bf16[16,32,16,128]{3,2,1,0:T(8,128)(2,1)} %dynamic-slice_bitcast_fusion), channel_id=1, source_target_pairs={{0,4},{4,0},{1,5},{5,1},{2,6},{6,2},{3,7},{7,3},{8,12},{12,8},{9,1... | collective-permute-start | bytes 6291464 | tf_op jit(solution)/shard_map/ppermute | solution.py:375
  185.9 31.1 %copy-start.6 = (f32[512,512]{1,0:T(8,128)S(1)}, f32[512,512]{1,0:T(8,128)}, u32[]{:S(2)}) copy-start(f32[512,512]{1,0:T(8,128)} %param.9) | copy-start | bytes 3145732
  210.1 42.6 %copy-start.3 = (bf16[16,64,512]{2,1,0:T(8,128)(2,1)}, bf16[16,64,512]{2,1,0:T(8,128)(2,1)S(1)}, u32[]{:S(2)}) copy-start(bf16[16,64,512]{2,1,0:T(8,128)(2,1)S(1)} %all_to_all.30) | copy-start | bytes 3145732
  211.3 24.8 %all-to-all-start.3 = ((bf16[16,64,512]{2,1,0:T(8,128)(2,1)}), bf16[16,64,512]{2,1,0:T(8,128)(2,1)}, u32[]{:S(2)}, u32[]{:S(2)}) async-start(bf16[16,64,512]{2,1,0:T(8,128)(2,1)} %broadcast_in_dim.4), calls=%async_computation.3 | async-start | bytes 2097152 | tf_op jit(solution)/shard_map/all_to_all | solution.py:354
  236.0 42.6 %collective-permute-start.1 = (bf16[16,32,16,128]{3,2,1,0:T(8,128)(2,1)}, bf16[16,32,16,128]{3,2,1,0:T(8,128)(2,1)}, u32[]{:S(2)}, u32[]{:S(2)}) collective-permute-start(bf16[16,32,16,128]{3,2,1,0:T(8,128)(2,1)} %get-tuple-element.21), channel_id=1, source_target_pairs={{0,4},{4,0},{1,5},{5,1},{2,6},{6,2},{3,7},{7,3},{8,12},{12,8},{9,1... | collective-permute-start | bytes 6291464 | tf_op jit(solution)/shard_map/ppermute | solution.py:409
  236.0 37.9 %all-to-all-start.5 = ((bf16[16,32,16,128]{3,2,1,0:T(8,128)(2,1)}), bf16[16,32,16,128]{3,2,1,0:T(8,128)(2,1)S(1)}, u32[]{:S(2)}, u32[]{:S(2)}) async-start(bf16[16,32,16,128]{3,2,1,0:T(8,128)(2,1)} %get-tuple-element.28), calls=%async_computation.5 | async-start | bytes 4194304 | tf_op jit(solution)/shard_map/all_to_all | solution.py:354
  248.8 57.9 %collective-permute-start.9 = (bf16[1024,512]{1,0:T(8,128)(2,1)}, bf16[1024,512]{1,0:T(8,128)(2,1)}, u32[]{:S(2)}, u32[]{:S(2)}) collective-permute-start(bf16[1024,512]{1,0:T(8,128)(2,1)} %bitcast.23.own), channel_id=1, source_target_pairs={{0,1},{1,0},{2,3},{3,2},{4,5},{5,4},{6,7},{7,6},{8,9},{9,8},{10,11... | collective-permute-start | bytes 3145736 | tf_op jit(solution)/shard_map/ppermute | solution.py:346
  252.7 70.6 %collective-permute-start.11 = (bf16[1024,512]{1,0:T(8,128)(2,1)S(1)}, bf16[1024,512]{1,0:T(8,128)(2,1)}, u32[]{:S(2)}, u32[]{:S(2)}) collective-permute-start(bf16[1024,512]{1,0:T(8,128)(2,1)S(1)} %bitcast.78), channel_id=1, source_target_pairs={{0,1},{1,0},{2,3},{3,2},{4,5},{5,4},{6,7},{7,6},{8,9},{9,8},{10,11... | collective-permute-start | bytes 3145736 | tf_op jit(solution)/shard_map/ppermute | solution.py:346
  273.9 4.7 %copy-start.5 = (bf16[16,32,16,128]{3,2,1,0:T(8,128)(2,1)}, bf16[16,32,16,128]{3,2,1,0:T(8,128)(2,1)S(1)}, u32[]{:S(2)}) copy-start(bf16[16,32,16,128]{3,2,1,0:T(8,128)(2,1)S(1)} %all-to-all-done.5.t) | copy-start | bytes 6291460
  278.6 111.9 %all-to-all-start.1 = ((bf16[16,32,16,128]{3,2,1,0:T(8,128)(2,1)}), bf16[16,32,16,128]{3,2,1,0:T(8,128)(2,1)S(1)}, u32[]{:S(2)}, u32[]{:S(2)}) async-start(bf16[16,32,16,128]{3,2,1,0:T(8,128)(2,1)} %collective-permute-done.1), calls=%async_computation.1 | async-start | bytes 4194304 | tf_op jit(solution)/shard_map/all_to_all | solution.py:354
  318.9 17.8 %copy-start.11 = (f32[512]{0:T(512)S(1)}, f32[512]{0:T(512)}, u32[]{:S(2)}) copy-start(f32[512]{0:T(512)} %param.13) | copy-start | bytes 6148
  318.9 63.8 %collective-permute-start.10 = (bf16[2,2048,128]{2,1,0:T(8,128)(2,1)}, bf16[2,2048,128]{2,1,0:T(8,128)(2,1)}, u32[]{:S(2)}, u32[]{:S(2)}) collective-permute-start(bf16[2,2048,128]{2,1,0:T(8,128)(2,1)} %get-tuple-element.23), channel_id=1, source_target_pairs={{0,1},{1,0},{2,3},{3,2},{4,5},{5,4},{6,7},{7,6},{8,9},{9,8},{10,11... | collective-permute-start | bytes 3145736 | tf_op jit(solution)/shard_map/ppermute | solution.py:346
  333.6 49.1 %collective-permute-start.13 = (bf16[2,1536,128]{2,1,0:T(8,128)(2,1)}, bf16[2,1536,128]{2,1,0:T(8,128)(2,1)S(1)}, u32[]{:S(2)}, u32[]{:S(2)}) collective-permute-start(bf16[2,1536,128]{2,1,0:T(8,128)(2,1)} %get-tuple-element.25), channel_id=1, source_target_pairs={{0,2},{1,3},{2,0},{3,1},{4,6},{5,7},{6,4},{7,5},{8,10},{9,11},{10,... | collective-permute-start | bytes 2359304 | tf_op jit(solution)/shard_map/ppermute | solution.py:346
  333.6 49.1 %collective-permute-start.15 = (bf16[2,1536,128]{2,1,0:T(8,128)(2,1)}, bf16[2,1536,128]{2,1,0:T(8,128)(2,1)}, u32[]{:S(2)}, u32[]{:S(2)}) collective-permute-start(bf16[2,1536,128]{2,1,0:T(8,128)(2,1)} %get-tuple-element.27), channel_id=1, source_target_pairs={{0,3},{1,2},{2,1},{3,0},{4,7},{5,6},{6,5},{7,4},{8,11},{9,10},{10,... | collective-permute-start | bytes 2359304 | tf_op jit(solution)/shard_map/ppermute | solution.py:346
  345.7 31.3 %collective-permute-start.12 = (bf16[2,512,128]{2,1,0:T(8,128)(2,1)}, bf16[2,512,128]{2,1,0:T(8,128)(2,1)S(1)}, u32[]{:S(2)}, u32[]{:S(2)}) collective-permute-start(bf16[2,512,128]{2,1,0:T(8,128)(2,1)} %get-tuple-element.24), channel_id=1, source_target_pairs={{0,2},{1,3},{2,0},{3,1},{4,6},{5,7},{6,4},{7,5},{8,10},{9,11},{10,... | collective-permute-start | bytes 786440 | tf_op jit(solution)/shard_map/ppermute | solution.py:346
  345.7 37.0 %collective-permute-start.14 = (bf16[2,512,128]{2,1,0:T(8,128)(2,1)}, bf16[2,512,128]{2,1,0:T(8,128)(2,1)S(1)}, u32[]{:S(2)}, u32[]{:S(2)}) collective-permute-start(bf16[2,512,128]{2,1,0:T(8,128)(2,1)} %get-tuple-element.26), channel_id=1, source_target_pairs={{0,3},{1,2},{2,1},{3,0},{4,7},{5,6},{6,5},{7,4},{8,11},{9,10},{10,... | collective-permute-start | bytes 786440 | tf_op jit(solution)/shard_map/ppermute | solution.py:346
  376.9 5.8 %copy-start.9 = (bf16[2,512,128]{2,1,0:T(8,128)(2,1)}, bf16[2,512,128]{2,1,0:T(8,128)(2,1)S(1)}, u32[]{:S(2)}) copy-start(bf16[2,512,128]{2,1,0:T(8,128)(2,1)S(1)} %collective-permute-done.12) | copy-start | bytes 786436
  382.7 0.7 copy-start.10
  382.7 1.0 copy-start.8
  390.5 1.4 copy-start.4

commit v2 on v0

--- a/solution.py
+++ b/solution.py
@@ -234,14 +234,17 @@
 
 
 def second(me, lt, own, oth, pieces, ham, far, first, steps):
+    def which(t, me):
+        return (0, 1 - me[0] // 2 if far else me[0] // 2)
+
     return call(
         functools.partial(second_body, far),
         (shape((2, steps * 512, 128)),) * 2,
         (steps,),
         [
             pl.BlockSpec((512, 2048), lambda t, me: (t + first, 0)),
-            whole((1024, 512)),
-            whole((1024, 512)),
+            pl.BlockSpec((1024, 512), which),
+            pl.BlockSpec((1024, 512), which),
         ]
         + [pl.BlockSpec((2, 512, 128), lambda t, me: (0, t + first, 0))] * 4
         + [whole((512, 512))],
@@ -399,13 +402,9 @@
     shares = [share] + [across(share, s) for s in (1, 2, 3)]
     aux = sum(v.astype(F32) for v in shares).astype(BF16)
 
-    half = lax.axis_index("zh")
-    far = lax.dynamic_slice_in_dim(aux, (1 - half) * 512, 512, 1)
-    near = lax.dynamic_slice_in_dim(aux, half * 512, 512, 1)
-    far = to_owner(jnp.broadcast_to(far[None], (16, 64, 512)), plane).reshape(1024, 512)
-    far_oth = swap(far, 1)
-    near = to_owner(jnp.broadcast_to(near[None], (16, 64, 512)), plane).reshape(1024, 512)
-    near_oth = swap(near, 1)
+    aux = jnp.broadcast_to(aux[None], (16, 64, 1024))
+    own = to_owner(aux, plane).reshape(1024, 1024)
+    oth = swap(own, 1)
 
     mixed_own, mixed_oth = mix(me, part_own, part_oth, ham)
     mixed_oth = lax.ppermute(mixed_oth, "zl", [(0, 1), (1, 0)])
@@ -414,9 +413,9 @@
 
     out_far = []
     for h in range(2):
-        r2, r3 = second(me, lt, far, far_oth, w, ham, True, h, 1 + 2 * h)
+        r2, r3 = second(me, lt, own, oth, w, ham, True, h, 1 + 2 * h)
         out_far.append((swap(r2, 2), swap(r3, 3)))
-    r0, r1 = second(me, lt, near, near_oth, w, ham, False, 0, 4)
+    r0, r1 = second(me, lt, own, oth, w, ham, False, 0, 4)
     r1 = swap(r1, 1)
     pieces = [r0, r1, *[out_far[h][s] for s in range(2) for h in range(2)]]
     out = finish(me, b, term_own, pieces, False, None)

time: 374 us -> 384 us (1.027)
  waiting for transfers between devices: 124 us -> 150 us
  blocking collectives: 17.5 us -> 0 us
    ppermute x3, waiting for transfers between devices: 4.7 us -> 44.9 us  [across(): return lax.ppermute(v, ('zl', 'zh'), [(d, d ^ s) for d in range(4)])]
    all_to_all x1 -> x0, blocking collectives: 17.5 us -> none  [to_owner(): return lax.all_to_all(v, axes, split_axis=0, concat_axis=0, tiled=True)]
    ppermute x1, waiting for transfers between devices: 13.8 us -> 0.01 us  [per_device(): mixed_oth = lax.ppermute(mixed_oth, 'zl', [(0, 1), (1, 0)])]
    ppermute x11 -> x10, starting transfers between devices: 26.6 us -> 23.2 us  [swap(): return lax.ppermute(v, ('zh', 'c'), [(d, d ^ s) for d in range(4)])]
    unnamed x28 -> x26, local copies, waits for them, and re-layouts: 7.32 us -> 7.92 us
    ppermute x11 -> x10, waiting for transfers between devices: 41.5 us -> 41.8 us  [swap(): return lax.ppermute(v, ('zh', 'c'), [(d, d ^ s) for d in range(4)])]
  transfers between devices with their start and end apart: 22 -> 21, of which waited for: 12 -> 10; matrix products, arithmetic and copies ran while one was open for 7% -> 7% of each run, Pallas kernels for 30% -> 29%
where the time goes in v2:
time: 384 us; the launch traced here: 381 us
  waiting for transfers between devices  150 us (39%)
  Pallas kernels  133 us (35%)
  starting transfers between devices  66 us (17%)
  local copies, waits for them, and re-layouts  13.7 us (4%)
  other arithmetic  10.6 us (3%)
  matrix products  6.7 us (2%)
    all_to_all x6, waiting for transfers between devices, to_owner(): return lax.all_to_all(v, axes, split_axis=0, concat_axis=0, tiled=True)  63.4 us
    ppermute x3, waiting for transfers between devices, across(): return lax.ppermute(v, ('zl', 'zh'), [(d, d ^ s) for d in range(4)])  44.9 us
    ppermute x10, waiting for transfers between devices, swap(): return lax.ppermute(v, ('zh', 'c'), [(d, d ^ s) for d in range(4)])  41.8 us
    all_to_all x6, starting transfers between devices, to_owner(): return lax.all_to_all(v, axes, split_axis=0, concat_axis=0, tiled=True)  38.6 us
    pallas_call x3, Pallas kernels, second(): call(functools.partial(second_body, far), (shape((2, steps * 512, 128)),)...  28.7 us
    ppermute x10, starting transfers between devices, swap(): return lax.ppermute(v, ('zh', 'c'), [(d, d ^ s) for d in range(4)])  23.2 us
    pallas_call x2, Pallas kernels, project(): call(project_body, shape((1024, 1024), dtype), (2,), [pl.BlockSpec((512,...  21.5 us
    pallas_call x1, Pallas kernels, base(): call(base_body, shape((2, 16, 512, 128), F32), (16,), [pl.BlockSpec((2, 1...  14.4 us
  transfers between devices with their start and end apart: 21, of which 10 were waited for; matrix products, arithmetic and copies ran while one was open for 7% of the time, Pallas kernels for 29%

profile of v2, /device:TPU:1, one launch (start us, length us, event | category | flops | bytes accessed | tf_op | source)
XLA Modules:
  0.0 381.0 jit_solution(13934533805813311382)
XLA Ops:
  0.6 5.0 %shard_map.73 = (bf16[2,16,128,128]{3,2,1,0:T(8,128)(2,1)}, bf16[2,16,128,128]{3,2,1,0:T(8,128)(2,1)}) custom-call(s32[2]{0:T(128)} %pad_add_fusion.me, bf16[16,1024,128]{2,1,0:T(8,128)(2,1)} %bitcast.49), custom_call_target="tpu_custom_call" | custom-call | flops 16777216 | bytes 4194304 | tf_op jit(solution)/shard_map/pallas_call | solution.py:61
  5.6 1.4 collective-permute-start.2
  7.0 5.0 %shard_map.74 = (bf16[2,16,128,128]{3,2,1,0:T(8,128)(2,1)}, bf16[2,16,128,128]{3,2,1,0:T(8,128)(2,1)}) custom-call(s32[2]{0:T(128)} %pad_add_fusion.me, bf16[16,1024,128]{2,1,0:T(8,128)(2,1)} %bitcast.50), custom_call_target="tpu_custom_call" | custom-call | flops 16777216 | bytes 4194304 | tf_op jit(solution)/shard_map/pallas_call | solution.py:61
  12.0 3.7 collective-permute-start.3
  16.4 14.4 %shard_map.79.la = bf16[2048,2048]{1,0:T(8,128)(2,1)} custom-call(s32[2]{0:T(128)} %pad_add_fusion.me, bf16[2048,16,128]{2,1,0:T(8,128)(2,1)} %l.1), custom_call_target="tpu_custom_call" | custom-call | flops 16777216 | bytes 16777216 | tf_op jit(solution)/shard_map/pallas_call | solution.py:112
  32.2 6.7 %fusion.2.z = f32[2048,2]{1,0:T(8,128)} fusion(bf16[2048,16,128]{2,1,0:T(8,128)(2,1)} %l.1, bf16[2,16,128]{2,1,0:T(8,128)(2,1)S(1)} %constant_dynamic-slice_fusion), kind=kOutput, calls=%fused_computation.3 | convolution fusion | flops 16777216 | bytes 8413184 | tf_op jit(solution)/shard_map/dot_general | solution.py:386
  39.4 22.5 %collective-permute-done.4 = bf16[2,16,128,128]{3,2,1,0:T(8,128)(2,1)S(1)} collective-permute-done((bf16[2,16,128,128]{3,2,1,0:T(8,128)(2,1)}, bf16[2,16,128,128]{3,2,1,0:T(8,128)(2,1)S(1)}, u32[]{:S(2)}, u32[]{:S(2)}) %collective-permute-start.4) | collective-permute-done | bytes 1048608 | tf_op jit(solution)/shard_map/ppermute | solution.py:350
  61.9 1.0 copy-done.3
  62.8 10.6 %shard_map.82 = bf16[1024,1024]{1,0:T(8,128)(2,1)} custom-call(s32[2]{0:T(128)} %pad_add_fusion.me, bf16[2048,2048]{1,0:T(8,128)(2,1)} %shard_map.79.la, bf16[2,2048,128]{2,1,0:T(8,128)(2,1)} %bitcast.65, bf16[2,2048,128]{2,1,0:T(8,128)(2,1)} %bitcast.70, bf16[2,2048,128]{2,1,0:T(8,128)(2,1)} %bitcast.75, bf16[2,2048,128]{2,1,0:T(8,128)(2,1)} %bitcast.80, ...), custom_call_target="tpu_custom_call" | custom-call | flops 4294967296 | bytes 10485760 | tf_op jit(solution)/shard_map/pallas_call | solution.py:198
  73.8 5.0 %shard_map.77 = bf16[16,32,16,128]{3,2,1,0:T(8,128)(2,1)} custom-call(s32[2]{0:T(128)} %pad_add_fusion.me, bf16[16,1024,128]{2,1,0:T(8,128)(2,1)} %bitcast.51, bf16[16,1024,128]{2,1,0:T(8,128)(2,1)} %bitcast.52, bf16[16,1024,128]{2,1,0:T(8,128)(2,1)} %bitcast.53, bf16[16,1024,128]{2,1,0:T(8,128)(2,1)} %bitcast.54), custom_call_target="tpu_custom_call" | custom-call | flops 16777216 | bytes 4194304 | tf_op jit(solution)/shard_map/pallas_call | solution.py:91
  78.8 6.8 %all-to-all-start.1 = ((bf16[16,32,16,128]{3,2,1,0:T(8,128)(2,1)}), bf16[16,32,16,128]{3,2,1,0:T(8,128)(2,1)S(1)}, u32[]{:S(2)}, u32[]{:S(2)}) async-start(bf16[16,32,16,128]{3,2,1,0:T(8,128)(2,1)} %shard_map.77), calls=%async_computation.1 | async-start | bytes 4194304 | tf_op jit(solution)/shard_map/all_to_all | solution.py:358
  85.5 10.9 %shard_map.81 = f32[1024,1024]{1,0:T(8,128)} custom-call(s32[2]{0:T(128)} %pad_add_fusion.me, bf16[2048,2048]{1,0:T(8,128)(2,1)} %shard_map.79.la, bf16[2,2048,128]{2,1,0:T(8,128)(2,1)} %bitcast.66, bf16[2,2048,128]{2,1,0:T(8,128)(2,1)} %bitcast.71, bf16[2,2048,128]{2,1,0:T(8,128)(2,1)} %bitcast.76, bf16[2,2048,128]{2,1,0:T(8,128)(2,1)} %bitcast.81, ...), custom_call_target="tpu_custom_call" | custom-call | flops 4294967296 | bytes 10485760 | tf_op jit(solution)/shard_map/pallas_call | solution.py:198
  96.5 5.0 %add_convert_fusion = bf16[1024,1024]{1,0:T(8,128)(2,1)} fusion(f32[1024,1024]{1,0:T(8,128)} %shard_map.81, bf16[1024,1024]{1,0:T(8,128)(2,1)} %collective-permute-done.5), kind=kLoop, calls=%fused_computation.2 | loop fusion | flops 3145728 | bytes 8388608 | tf_op jit(solution)/shard_map/convert_element_type | solution.py:399
  101.5 13.2 %all-to-all-done.1 = bf16[16,32,16,128]{3,2,1,0:T(8,128)(2,1)S(1)} async-done(((bf16[16,32,16,128]{3,2,1,0:T(8,128)(2,1)}), bf16[16,32,16,128]{3,2,1,0:T(8,128)(2,1)S(1)}, u32[]{:S(2)}, u32[]{:S(2)}) %all-to-all-start.1) | async-done | bytes 2097184 | tf_op jit(solution)/shard_map/all_to_all | solution.py:358
  114.7 1.3 copy-done.8
  116.0 5.4 %all-to-all-start.3 = ((bf16[16,64,1024]{2,1,0:T(8,128)(2,1)}), bf16[16,64,1024]{2,1,0:T(8,128)(2,1)S(1)}, u32[]{:S(2)}, u32[]{:S(2)}) async-start(bf16[16,64,1024]{2,1,0:T(8,128)(2,1)} %bitcast.85), calls=%async_computation.3 | async-start | bytes 4194304 | tf_op jit(solution)/shard_map/all_to_all | solution.py:358
  121.4 5.0 %shard_map.76 = bf16[16,32,16,128]{3,2,1,0:T(8,128)(2,1)} custom-call(s32[2]{0:T(128)} %pad_add_fusion.me, bf16[16,1024,128]{2,1,0:T(8,128)(2,1)} %bitcast.55, bf16[16,1024,128]{2,1,0:T(8,128)(2,1)} %bitcast.56, bf16[16,1024,128]{2,1,0:T(8,128)(2,1)} %bitcast.57, bf16[16,1024,128]{2,1,0:T(8,128)(2,1)} %bitcast.58), custom_call_target="tpu_custom_call" | custom-call | flops 16777216 | bytes 4194304 | tf_op jit(solution)/shard_map/pallas_call | solution.py:91
  126.4 20.8 %all-to-all-done.3 = bf16[16,64,1024]{2,1,0:T(8,128)(2,1)S(1)} async-done(((bf16[16,64,1024]{2,1,0:T(8,128)(2,1)}), bf16[16,64,1024]{2,1,0:T(8,128)(2,1)S(1)}, u32[]{:S(2)}, u32[]{:S(2)}) %all-to-all-start.3) | async-done | bytes 2097184 | tf_op jit(solution)/shard_map/all_to_all | solution.py:358
  147.2 5.6 %all-to-all-start = ((bf16[16,32,16,128]{3,2,1,0:T(8,128)(2,1)}), bf16[16,32,16,128]{3,2,1,0:T(8,128)(2,1)}, u32[]{:S(2)}, u32[]{:S(2)}) async-start(bf16[16,32,16,128]{3,2,1,0:T(8,128)(2,1)} %shard_map.76), calls=%async_computation | async-start | bytes 4194304 | tf_op jit(solution)/shard_map/all_to_all | solution.py:358
  153.5 3.4 collective-permute-start.6
  157.3 43.5 %collective-permute-done.6 = bf16[64,1024]{1,0:T(8,128)(2,1)S(1)} collective-permute-done((bf16[64,1024]{1,0:T(8,128)(2,1)S(1)}, bf16[64,1024]{1,0:T(8,128)(2,1)S(1)}, u32[]{:S(2)}, u32[]{:S(2)}) %collective-permute-start.6) | collective-permute-done | bytes 131104 | tf_op jit(solution)/shard_map/ppermute | solution.py:354
  200.8 1.4 collective-permute-done.7
  202.3 1.6 broadcast_in_dim.2
  203.9 6.1 %all-to-all-start.4 = ((bf16[16,64,1024]{2,1,0:T(8,128)(2,1)}), bf16[16,64,1024]{2,1,0:T(8,128)(2,1)S(1)}, u32[]{:S(2)}, u32[]{:S(2)}) async-start(bf16[16,64,1024]{2,1,0:T(8,128)(2,1)} %broadcast_in_dim.2), calls=%async_computation.4 | async-start | bytes 4194304 | tf_op jit(solution)/shard_map/all_to_all | solution.py:358
  210.0 2.7 copy.17
  212.7 1.3 copy.18
  214.7 3.2 fusion.7.ham
  217.9 6.9 %shard_map.78 = (bf16[16,32,16,128]{3,2,1,0:T(8,128)(2,1)}, bf16[16,32,16,128]{3,2,1,0:T(8,128)(2,1)}) custom-call(s32[2]{0:T(128)} %pad_add_fusion.me, bf16[16,32,16,128]{3,2,1,0:T(8,128)(2,1)} %all-to-all-done.own, bf16[16,32,16,128]{3,2,1,0:T(8,128)(2,1)} %collective-permute-done.oth, bf16[512,512]{1,0:T(8,128)(2,1)} %fusion.7.ham), custom_call_target="tpu_custom_call" | custom-call | flops 2147483648 | bytes 8388608 | tf_op jit(solution)/shard_map/pallas_call | solution.py:276
  224.8 8.5 %all-to-all-done.4 = bf16[16,64,1024]{2,1,0:T(8,128)(2,1)S(1)} async-done(((bf16[16,64,1024]{2,1,0:T(8,128)(2,1)}), bf16[16,64,1024]{2,1,0:T(8,128)(2,1)S(1)}, u32[]{:S(2)}, u32[]{:S(2)}) %all-to-all-start.4) | async-done | bytes 2097184 | tf_op jit(solution)/shard_map/all_to_all | solution.py:358
  233.3 8.4 %all-to-all-start.5 = ((bf16[16,32,16,128]{3,2,1,0:T(8,128)(2,1)}), bf16[16,32,16,128]{3,2,1,0:T(8,128)(2,1)}, u32[]{:S(2)}, u32[]{:S(2)}) async-start(bf16[16,32,16,128]{3,2,1,0:T(8,128)(2,1)} %get-tuple-element.28), calls=%async_computation.5 | async-start | bytes 4194304 | tf_op jit(solution)/shard_map/all_to_all | solution.py:358
  241.6 4.1 %collective-permute-start.9 = (bf16[1024,1024]{1,0:T(8,128)(2,1)S(1)}, bf16[1024,1024]{1,0:T(8,128)(2,1)}, u32[]{:S(2)}, u32[]{:S(2)}) collective-permute-start(bf16[1024,1024]{1,0:T(8,128)(2,1)S(1)} %bitcast.61), channel_id=1, source_target_pairs={{0,1},{1,0},{2,3},{3,2},{4,5},{5,4},{6,7},{7,6},{8,9},{9,8},{10,11... | collective-permute-start | bytes 6291464 | tf_op jit(solution)/shard_map/ppermute | solution.py:350
  245.7 21.0 %all-to-all-done.5.t = bf16[16,32,16,128]{3,2,1,0:T(8,128)(2,1)} async-done(((bf16[16,32,16,128]{3,2,1,0:T(8,128)(2,1)}), bf16[16,32,16,128]{3,2,1,0:T(8,128)(2,1)}, u32[]{:S(2)}, u32[]{:S(2)}) %all-to-all-start.5) | async-done | bytes 2097184 | tf_op jit(solution)/shard_map/all_to_all | solution.py:358
  266.7 6.3 %all-to-all-start.2 = ((bf16[16,32,16,128]{3,2,1,0:T(8,128)(2,1)}), bf16[16,32,16,128]{3,2,1,0:T(8,128)(2,1)}, u32[]{:S(2)}, u32[]{:S(2)}) async-start(bf16[16,32,16,128]{3,2,1,0:T(8,128)(2,1)} %collective-permute-done.1), calls=%async_computation.2 | async-start | bytes 4194304 | tf_op jit(solution)/shard_map/all_to_all | solution.py:358
  273.0 13.9 %shard_map.80.lt = bf16[2048,2048]{1,0:T(8,128)(2,1)} custom-call(s32[2]{0:T(128)} %pad_add_fusion.me, bf16[2048,2048]{1,0:T(8,128)(2,1)} %shard_map.79.la), custom_call_target="tpu_custom_call" | custom-call | flops 67108864 | bytes 16777216 | tf_op jit(solution)/shard_map/pallas_call | solution.py:130
  286.9 12.3 %shard_map.83 = (bf16[2,2048,128]{2,1,0:T(8,128)(2,1)}, bf16[2,2048,128]{2,1,0:T(8,128)(2,1)}) custom-call(s32[2]{0:T(128)} %pad_add_fusion.me, bf16[2048,2048]{1,0:T(8,128)(2,1)} %shard_map.80.lt, bf16[1024,1024]{1,0:T(8,128)(2,1)} %bitcast.62, bf16[1024,1024]{1,0:T(8,128)(2,1)} %collective-permute-done.9.oth, bf16[2,2048,128]{2,1,0:T(8,128)(2,1)} %bitcast.67, ...), custom_call_target="tpu_custom_call" | custom-call | flops 2147483648 | bytes 8388608 | tf_op jit(solution)/shard_map/pallas_call | solution.py:240
  299.2 7.2 %collective-permute-start.10 = (bf16[2,2048,128]{2,1,0:T(8,128)(2,1)}, bf16[2,2048,128]{2,1,0:T(8,128)(2,1)S(1)}, u32[]{:S(2)}, u32[]{:S(2)}) collective-permute-start(bf16[2,2048,128]{2,1,0:T(8,128)(2,1)} %get-tuple-element.23), channel_id=1, source_target_pairs={{0,1},{1,0},{2,3},{3,2},{4,5},{5,4},{6,7},{7,6},{8,9},{9,8},{10,11... | collective-permute-start | bytes 3145736 | tf_op jit(solution)/shard_map/ppermute | solution.py:350
  306.4 10.4 %shard_map.85 = (bf16[2,1536,128]{2,1,0:T(8,128)(2,1)}, bf16[2,1536,128]{2,1,0:T(8,128)(2,1)}) custom-call(s32[2]{0:T(128)} %pad_add_fusion.me, bf16[2048,2048]{1,0:T(8,128)(2,1)} %shard_map.80.lt, bf16[1024,1024]{1,0:T(8,128)(2,1)} %bitcast.63, bf16[1024,1024]{1,0:T(8,128)(2,1)} %collective-permute-done.9.oth, bf16[2,2048,128]{2,1,0:T(8,128)(2,1)} %bitcast.68, ...), custom_call_target="tpu_custom_call" | custom-call | flops 2147483648 | bytes 8388608 | tf_op jit(solution)/shard_map/pallas_call | solution.py:240
  316.8 2.0 collective-permute-start.12
  318.7 1.2 collective-permute-start.14
  321.8 0.9 copy.19.dk
  322.7 6.1 %shard_map.84 = (bf16[2,512,128]{2,1,0:T(8,128)(2,1)}, bf16[2,512,128]{2,1,0:T(8,128)(2,1)}) custom-call(s32[2]{0:T(128)} %pad_add_fusion.me, bf16[2048,2048]{1,0:T(8,128)(2,1)} %shard_map.80.lt, bf16[1024,1024]{1,0:T(8,128)(2,1)} %bitcast.64, bf16[1024,1024]{1,0:T(8,128)(2,1)} %collective-permute-done.9.oth, bf16[2,2048,128]{2,1,0:T(8,128)(2,1)} %bitcast.69, ...), custom_call_target="tpu_custom_call" | custom-call | flops 2147483648 | bytes 8388608 | tf_op jit(solution)/shard_map/pallas_call | solution.py:240
  328.7 2.0 collective-permute-start.11
  330.7 1.4 collective-permute-start.13
  332.6 14.4 %shard_map.75 = f32[2,16,512,128]{3,2,1,0:T(8,128)} custom-call(s32[2]{0:T(128)} %pad_add_fusion.me, bf16[2,16,128,128]{3,2,1,0:T(8,128)(2,1)} %get-tuple-element.17.e0, bf16[2,16,128,128]{3,2,1,0:T(8,128)(2,1)} %get-tuple-element.18.e1, bf16[2,16,128,128]{3,2,1,0:T(8,128)(2,1)} %get-tuple-element.19.e2, bf16[2,16,128,128]{3,2,1,0:T(8,128)(2,1)} %get-tuple-element.20.e3, ...), custom_call_target="tpu_custom_call" | custom-call | flops 2147483648 | bytes 12582912 | tf_op jit(solution)/shard_map/pallas_call | solution.py:157
  347.1 13.0 %collective-permute-done.11 = bf16[2,512,128]{2,1,0:T(8,128)(2,1)S(1)} collective-permute-done((bf16[2,512,128]{2,1,0:T(8,128)(2,1)}, bf16[2,512,128]{2,1,0:T(8,128)(2,1)S(1)}, u32[]{:S(2)}, u32[]{:S(2)}) %collective-permute-start.11) | collective-permute-done | bytes 262176 | tf_op jit(solution)/shard_map/ppermute | solution.py:350
  360.0 5.8 %collective-permute-done.13 = bf16[2,512,128]{2,1,0:T(8,128)(2,1)S(1)} collective-permute-done((bf16[2,512,128]{2,1,0:T(8,128)(2,1)}, bf16[2,512,128]{2,1,0:T(8,128)(2,1)S(1)}, u32[]{:S(2)}, u32[]{:S(2)}) %collective-permute-start.13) | collective-permute-done | bytes 262176 | tf_op jit(solution)/shard_map/ppermute | solution.py:350
  367.4 6.8 %shard_map.86.refs_0_ = bf16[16,16,2,32,128]{4,3,2,1,0:T(8,128)(2,1)} custom-call(s32[2]{0:T(128)} %pad_add_fusion.me, f32[2,16,16,2,16,128]{5,4,3,2,1,0:T(8,128)} %bitcast.59, bf16[16,32,16,128]{3,2,1,0:T(8,128)(2,1)} %all-to-all-done.5.t, bf16[2,16,4,2,16,128]{5,4,3,2,1,0:T(8,128)(2,1)} %bitcast.86, bf16[2,16,4,2,16,128]{5,4,3,2,1,0:T(8,128)(2,1)} %bitcast.88, ...), custom_call_target="tpu_custom_call" | custom-call | flops 16777216 | bytes 10485760 | tf_op jit(solution)/shard_map/pallas_call | solution.py:324
  374.2 6.8 %shard_map.87 = bf16[16,16,2,32,128]{4,3,2,1,0:T(8,128)(2,1)} custom-call(s32[2]{0:T(128)} %pad_add_fusion.me, f32[2,16,16,2,16,128]{5,4,3,2,1,0:T(8,128)} %bitcast.60, bf16[16,32,16,128]{3,2,1,0:T(8,128)(2,1)} %all-to-all-done.2.t, bf16[2,16,4,2,16,128]{5,4,3,2,1,0:T(8,128)(2,1)} %bitcast.87, ...), custom_call_target="tpu_custom_call", output_to_operand_aliasing={{}: (9, {})} | custom-call | flops 16777216 | bytes 10485760 | tf_op jit(solution)/shard_map/pallas_call | solution.py:324
  (50 shorter events, 9.1 us)
Async XLA Ops:
  5.6 33.3 %collective-permute-start.2 = (bf16[2,16,128,128]{3,2,1,0:T(8,128)(2,1)}, bf16[2,16,128,128]{3,2,1,0:T(8,128)(2,1)S(1)}, u32[]{:S(2)}, u32[]{:S(2)}) collective-permute-start(bf16[2,16,128,128]{3,2,1,0:T(8,128)(2,1)} %get-tuple-element.18.e1), channel_id=1, source_target_pairs={{0,1},{1,0},{2,3},{3,2},{4,5},{5,4},{6,7},{7,6},{8,9},{9,8},{10,11... | collective-permute-start | bytes 3145736 | tf_op jit(solution)/shard_map/ppermute | solution.py:350
  12.0 27.4 %collective-permute-start.3 = (bf16[2,16,128,128]{3,2,1,0:T(8,128)(2,1)}, bf16[2,16,128,128]{3,2,1,0:T(8,128)(2,1)S(1)}, u32[]{:S(2)}, u32[]{:S(2)}) collective-permute-start(bf16[2,16,128,128]{3,2,1,0:T(8,128)(2,1)} %get-tuple-element.19.e2), channel_id=1, source_target_pairs={{0,2},{1,3},{2,0},{3,1},{4,6},{5,7},{6,4},{7,5},{8,10},{9,11},{10,... | collective-permute-start | bytes 3145736 | tf_op jit(solution)/shard_map/ppermute | solution.py:350
  15.7 46.2 %collective-permute-start.4 = (bf16[2,16,128,128]{3,2,1,0:T(8,128)(2,1)}, bf16[2,16,128,128]{3,2,1,0:T(8,128)(2,1)S(1)}, u32[]{:S(2)}, u32[]{:S(2)}) collective-permute-start(bf16[2,16,128,128]{3,2,1,0:T(8,128)(2,1)} %get-tuple-element.20.e3), channel_id=1, source_target_pairs={{0,3},{1,2},{2,1},{3,0},{4,7},{5,6},{6,5},{7,4},{8,11},{9,10},{10,... | collective-permute-start | bytes 3145736 | tf_op jit(solution)/shard_map/ppermute | solution.py:350
  38.9 23.0 %copy-start.1 = (bf16[2,16,128,128]{3,2,1,0:T(8,128)(2,1)}, bf16[2,16,128,128]{3,2,1,0:T(8,128)(2,1)S(1)}, u32[]{:S(2)}) copy-start(bf16[2,16,128,128]{3,2,1,0:T(8,128)(2,1)S(1)} %collective-permute-done.2) | copy-start | bytes 3145732
  39.4 22.5 %copy-start.2 = (bf16[2,16,128,128]{3,2,1,0:T(8,128)(2,1)}, bf16[2,16,128,128]{3,2,1,0:T(8,128)(2,1)S(1)}, u32[]{:S(2)}) copy-start(bf16[2,16,128,128]{3,2,1,0:T(8,128)(2,1)S(1)} %collective-permute-done.3) | copy-start | bytes 3145732
  61.9 1.0 copy-start.3
  73.4 23.0 %collective-permute-start.5 = (bf16[1024,1024]{1,0:T(8,128)(2,1)}, bf16[1024,1024]{1,0:T(8,128)(2,1)}, u32[]{:S(2)}, u32[]{:S(2)}) collective-permute-start(bf16[1024,1024]{1,0:T(8,128)(2,1)} %shard_map.82), channel_id=1, source_target_pairs={{0,1},{1,0},{2,3},{3,2},{4,5},{5,4},{6,7},{7,6},{8,9},{9,8},{10,11... | collective-permute-start | bytes 6291464 | tf_op jit(solution)/shard_map/ppermute | solution.py:350
  78.8 35.9 %all-to-all-start.1 = ((bf16[16,32,16,128]{3,2,1,0:T(8,128)(2,1)}), bf16[16,32,16,128]{3,2,1,0:T(8,128)(2,1)S(1)}, u32[]{:S(2)}, u32[]{:S(2)}) async-start(bf16[16,32,16,128]{3,2,1,0:T(8,128)(2,1)} %shard_map.77), calls=%async_computation.1 | async-start | bytes 4194304 | tf_op jit(solution)/shard_map/all_to_all | solution.py:358
  114.7 1.4 copy-start.8
  116.0 31.2 %all-to-all-start.3 = ((bf16[16,64,1024]{2,1,0:T(8,128)(2,1)}), bf16[16,64,1024]{2,1,0:T(8,128)(2,1)S(1)}, u32[]{:S(2)}, u32[]{:S(2)}) async-start(bf16[16,64,1024]{2,1,0:T(8,128)(2,1)} %bitcast.85), calls=%async_computation.3 | async-start | bytes 4194304 | tf_op jit(solution)/shard_map/all_to_all | solution.py:358
  147.2 55.1 %all-to-all-start = ((bf16[16,32,16,128]{3,2,1,0:T(8,128)(2,1)}), bf16[16,32,16,128]{3,2,1,0:T(8,128)(2,1)}, u32[]{:S(2)}, u32[]{:S(2)}) async-start(bf16[16,32,16,128]{3,2,1,0:T(8,128)(2,1)} %shard_map.76), calls=%async_computation | async-start | bytes 4194304 | tf_op jit(solution)/shard_map/all_to_all | solution.py:358
  152.7 65.1 %collective-permute-start = (bf16[16,32,16,128]{3,2,1,0:T(8,128)(2,1)}, bf16[16,32,16,128]{3,2,1,0:T(8,128)(2,1)}, u32[]{:S(2)}, u32[]{:S(2)}) collective-permute-start(bf16[16,32,16,128]{3,2,1,0:T(8,128)(2,1)} %copy-done.8), channel_id=1, source_target_pairs={{0,4},{4,0},{1,5},{5,1},{2,6},{6,2},{3,7},{7,3},{8,12},{12,8},{9,1... | collective-permute-start | bytes 6291464 | tf_op jit(solution)/shard_map/ppermute | solution.py:378
  153.5 47.3 %collective-permute-start.6 = (bf16[64,1024]{1,0:T(8,128)(2,1)S(1)}, bf16[64,1024]{1,0:T(8,128)(2,1)S(1)}, u32[]{:S(2)}, u32[]{:S(2)}) collective-permute-start(bf16[64,1024]{1,0:T(8,128)(2,1)S(1)} %reduce_sum.12), channel_id=1, source_target_pairs={{0,2},{2,0},{4,6},{6,4},{1,3},{3,1},{5,7},{7,5},{8,10},{10,8},{12,... | collective-permute-start | bytes 393224 | tf_op jit(solution)/shard_map/ppermute | solution.py:354
  156.9 45.3 %collective-permute-start.7 = (bf16[64,1024]{1,0:T(8,128)(2,1)S(1)}, bf16[64,1024]{1,0:T(8,128)(2,1)S(1)}, u32[]{:S(2)}, u32[]{:S(2)}) collective-permute-start(bf16[64,1024]{1,0:T(8,128)(2,1)S(1)} %reduce_sum.12), channel_id=1, source_target_pairs={{0,4},{2,6},{4,0},{6,2},{1,5},{3,7},{5,1},{7,3},{8,12},{10,14},{12... | collective-permute-start | bytes 393224 | tf_op jit(solution)/shard_map/ppermute | solution.py:354
  156.9 45.3 %collective-permute-start.8 = (bf16[64,1024]{1,0:T(8,128)(2,1)S(1)}, bf16[64,1024]{1,0:T(8,128)(2,1)S(1)}, u32[]{:S(2)}, u32[]{:S(2)}) collective-permute-start(bf16[64,1024]{1,0:T(8,128)(2,1)S(1)} %reduce_sum.12), channel_id=1, source_target_pairs={{0,6},{2,4},{4,2},{6,0},{1,7},{3,5},{5,3},{7,1},{8,14},{10,12},{12... | collective-permute-start | bytes 393224 | tf_op jit(solution)/shard_map/ppermute | solution.py:354
  203.9 29.4 %all-to-all-start.4 = ((bf16[16,64,1024]{2,1,0:T(8,128)(2,1)}), bf16[16,64,1024]{2,1,0:T(8,128)(2,1)S(1)}, u32[]{:S(2)}, u32[]{:S(2)}) async-start(bf16[16,64,1024]{2,1,0:T(8,128)(2,1)} %broadcast_in_dim.2), calls=%async_computation.4 | async-start | bytes 4194304 | tf_op jit(solution)/shard_map/all_to_all | solution.py:358
  210.0 2.7 copy-start.4
  224.8 41.9 %collective-permute-start.1 = (bf16[16,32,16,128]{3,2,1,0:T(8,128)(2,1)}, bf16[16,32,16,128]{3,2,1,0:T(8,128)(2,1)}, u32[]{:S(2)}, u32[]{:S(2)}) collective-permute-start(bf16[16,32,16,128]{3,2,1,0:T(8,128)(2,1)} %get-tuple-element.21), channel_id=1, source_target_pairs={{0,4},{4,0},{1,5},{5,1},{2,6},{6,2},{3,7},{7,3},{8,12},{12,8},{9,1... | collective-permute-start | bytes 6291464 | tf_op jit(solution)/shard_map/ppermute | solution.py:410
  233.2 8.4 %copy-start = (bf16[16,64,1024]{2,1,0:T(8,128)(2,1)}, bf16[16,64,1024]{2,1,0:T(8,128)(2,1)S(1)}, u32[]{:S(2)}) copy-start(bf16[16,64,1024]{2,1,0:T(8,128)(2,1)S(1)} %all-to-all-done.4) | copy-start | bytes 6291460
  233.3 33.5 %all-to-all-start.5 = ((bf16[16,32,16,128]{3,2,1,0:T(8,128)(2,1)}), bf16[16,32,16,128]{3,2,1,0:T(8,128)(2,1)}, u32[]{:S(2)}, u32[]{:S(2)}) async-start(bf16[16,32,16,128]{3,2,1,0:T(8,128)(2,1)} %get-tuple-element.28), calls=%async_computation.5 | async-start | bytes 4194304 | tf_op jit(solution)/shard_map/all_to_all | solution.py:358
  241.6 45.3 %collective-permute-start.9 = (bf16[1024,1024]{1,0:T(8,128)(2,1)S(1)}, bf16[1024,1024]{1,0:T(8,128)(2,1)}, u32[]{:S(2)}, u32[]{:S(2)}) collective-permute-start(bf16[1024,1024]{1,0:T(8,128)(2,1)S(1)} %bitcast.61), channel_id=1, source_target_pairs={{0,1},{1,0},{2,3},{3,2},{4,5},{5,4},{6,7},{7,6},{8,9},{9,8},{10,11... | collective-permute-start | bytes 6291464 | tf_op jit(solution)/shard_map/ppermute | solution.py:350
  266.7 107.5 %all-to-all-start.2 = ((bf16[16,32,16,128]{3,2,1,0:T(8,128)(2,1)}), bf16[16,32,16,128]{3,2,1,0:T(8,128)(2,1)}, u32[]{:S(2)}, u32[]{:S(2)}) async-start(bf16[16,32,16,128]{3,2,1,0:T(8,128)(2,1)} %collective-permute-done.1), calls=%async_computation.2 | async-start | bytes 4194304 | tf_op jit(solution)/shard_map/all_to_all | solution.py:358
  299.2 20.7 %copy-start.11 = (f32[512]{0:T(512)S(1)}, f32[512]{0:T(512)}, u32[]{:S(2)}) copy-start(f32[512]{0:T(512)} %param.13) | copy-start | bytes 6148
  299.2 66.6 %collective-permute-start.10 = (bf16[2,2048,128]{2,1,0:T(8,128)(2,1)}, bf16[2,2048,128]{2,1,0:T(8,128)(2,1)S(1)}, u32[]{:S(2)}, u32[]{:S(2)}) collective-permute-start(bf16[2,2048,128]{2,1,0:T(8,128)(2,1)} %get-tuple-element.23), channel_id=1, source_target_pairs={{0,1},{1,0},{2,3},{3,2},{4,5},{5,4},{6,7},{7,6},{8,9},{9,8},{10,11... | collective-permute-start | bytes 3145736 | tf_op jit(solution)/shard_map/ppermute | solution.py:350
  316.8 49.1 %collective-permute-start.12 = (bf16[2,1536,128]{2,1,0:T(8,128)(2,1)}, bf16[2,1536,128]{2,1,0:T(8,128)(2,1)S(1)}, u32[]{:S(2)}, u32[]{:S(2)}) collective-permute-start(bf16[2,1536,128]{2,1,0:T(8,128)(2,1)} %get-tuple-element.25), channel_id=1, source_target_pairs={{0,2},{1,3},{2,0},{3,1},{4,6},{5,7},{6,4},{7,5},{8,10},{9,11},{10,... | collective-permute-start | bytes 2359304 | tf_op jit(solution)/shard_map/ppermute | solution.py:350
  318.7 47.1 %collective-permute-start.14 = (bf16[2,1536,128]{2,1,0:T(8,128)(2,1)}, bf16[2,1536,128]{2,1,0:T(8,128)(2,1)S(1)}, u32[]{:S(2)}, u32[]{:S(2)}) collective-permute-start(bf16[2,1536,128]{2,1,0:T(8,128)(2,1)} %get-tuple-element.27), channel_id=1, source_target_pairs={{0,3},{1,2},{2,1},{3,0},{4,7},{5,6},{6,5},{7,4},{8,11},{9,10},{10,... | collective-permute-start | bytes 2359304 | tf_op jit(solution)/shard_map/ppermute | solution.py:350
  328.7 31.3 %collective-permute-start.11 = (bf16[2,512,128]{2,1,0:T(8,128)(2,1)}, bf16[2,512,128]{2,1,0:T(8,128)(2,1)S(1)}, u32[]{:S(2)}, u32[]{:S(2)}) collective-permute-start(bf16[2,512,128]{2,1,0:T(8,128)(2,1)} %get-tuple-element.24), channel_id=1, source_target_pairs={{0,2},{1,3},{2,0},{3,1},{4,6},{5,7},{6,4},{7,5},{8,10},{9,11},{10,... | collective-permute-start | bytes 786440 | tf_op jit(solution)/shard_map/ppermute | solution.py:350
  330.7 35.1 %collective-permute-start.13 = (bf16[2,512,128]{2,1,0:T(8,128)(2,1)}, bf16[2,512,128]{2,1,0:T(8,128)(2,1)S(1)}, u32[]{:S(2)}, u32[]{:S(2)}) collective-permute-start(bf16[2,512,128]{2,1,0:T(8,128)(2,1)} %get-tuple-element.26), channel_id=1, source_target_pairs={{0,3},{1,2},{2,1},{3,0},{4,7},{5,6},{6,5},{7,4},{8,11},{9,10},{10,... | collective-permute-start | bytes 786440 | tf_op jit(solution)/shard_map/ppermute | solution.py:350
  360.0 5.8 %copy-start.9 = (bf16[2,512,128]{2,1,0:T(8,128)(2,1)}, bf16[2,512,128]{2,1,0:T(8,128)(2,1)S(1)}, u32[]{:S(2)}) copy-start(bf16[2,512,128]{2,1,0:T(8,128)(2,1)S(1)} %collective-permute-done.11) | copy-start | bytes 786436
  365.8 0.7 copy-start.10
  365.8 1.0 copy-start.6
  365.8 1.2 copy-start.7
  365.9 1.6 copy-start.5
